TPU v7x, 32 devices: a whole 2x2x4 slice. The times are simulated.
32 devices in a mesh: bank: 16 (over z, x, core), zero: 2 (over y).
Axes of the slice: x: 2, y: 2, z: 4, core: 2. Of those that a mesh axis runs over, the one named last changes fastest.
Arguments:
- master_down: float32 [64, 1408, 2048], P('bank', None, 'zero'), may hold values from -0.21875 to 0.21875
- second_down: bfloat16 [64, 1408, 2048], P('bank', None, 'zero'), may hold values from -0.078125 to 0.078125
- router_weight: float32 [2048, 64], P('zero', 'bank'), may hold values from -0.125 to 0.125
- router_gain: float32 [2048], P('zero'), may hold values from 0.25 to 1.75
Outputs:
- final_down: bfloat16 [64, 1408, 2048], P('bank')
- scale_down: float32 [64, 1408], P('bank')
- serve_router: bfloat16 [2048, 64], replicated
All inputs are finite; a program needn't handle non-finite values.
Results may differ from a plain program's by a relative error of at most 0.001.
Values may be sent and summed in bfloat16 or wider, within the bound.
No kernel may reach another device: no remote copies, remote signals or barrier semaphores. Data moves between devices by JAX's collectives and lax.ppermute only.
A program may use at most 128 MiB of HBM per device.

v0:
```python
import jax
import jax.numpy as jnp
from jax import lax
from jax.sharding import PartitionSpec as P


def body(master_down, second_down, router_weight, router_gain):
    merged_down = master_down + second_down.astype(jnp.float32)
    total_down = lax.psum(jnp.sum(merged_down * merged_down, axis=2), "zero")
    scale_down = jnp.sqrt(total_down)
    narrow_down = (merged_down / jnp.expand_dims(scale_down, 2)).astype(jnp.bfloat16)
    final_down = lax.all_gather(narrow_down, "zero", axis=2, tiled=True)
    part_router = (router_weight * router_gain[:, None]).astype(jnp.bfloat16)
    row_router = lax.all_gather(part_router, "zero", axis=0, tiled=True)
    serve_router = lax.all_gather(row_router, "bank", axis=1, tiled=True)
    return (final_down, scale_down, serve_router)


def solution(mesh):
    return jax.shard_map(
        body,
        mesh=mesh,
        in_specs=(P("bank", None, "zero"), P("bank", None, "zero"), P("zero", "bank"), P("zero")),
        out_specs=(P("bank", None, None), P("bank", None), P()),
        check_vma=False,
    )
```

profile of v0, /device:TPU:0, one launch (start us, length us, event | category | flops | bytes accessed | tf_op | source)
XLA Modules:
  0.0 344.6 jit_solution(7127730222345791311)
XLA Ops:
  7.2 0.0 all-gather.3.cloned.1.call-start
  7.2 12.6 %multiply_reduce_fusion = f32[4,1408]{1,0:T(4,128)S(1)} fusion(f32[4,1408,1024]{2,1,0:T(8,128)} %param.4, bf16[4,1408,1024]{2,1,0:T(8,128)(2,1)} %param.5), kind=kLoop, calls=%fused_computation.1 | loop fusion | flops 23063040 | bytes 34625536 | tf_op jit(solution)/shard_map/reduce_sum | solution.py:9
  19.8 9.9 %psum.7 = f32[4,1408]{1,0:T(4,128)S(1)} all-reduce(f32[4,1408]{1,0:T(4,128)S(1)} %multiply_reduce_fusion), channel_id=1, replica_groups=mesh['bank'=16,'zero'=2] {'zero'}, use_global_device_ids=true, to_apply=%region_1.0 | all-reduce | flops 5632 | bytes 45056 | tf_op jit(solution)/shard_map/psum | solution.py:9
  29.7 0.0 copy-start
  29.7 0.0 copy-start.1
  29.7 0.0 copy-start.2
  29.8 17.0 %divide_convert_fusion = bf16[4,1408,1024]{2,1,0:T(8,128)(2,1)} fusion(f32[4,1408,1024]{2,1,0:T(8,128)} %param.4, bf16[4,1408,1024]{2,1,0:T(8,128)(2,1)} %param.5, f32[4,1408]{1,0:T(4,128)S(1)} %sqrt.3), kind=kLoop, calls=%fused_computation | loop fusion | flops 23068672 | bytes 46159872 | tf_op jit(solution)/shard_map/convert_element_type | solution.py:11
  46.7 0.0 copy-done
  46.7 0.0 all-gather.3.cloned.1.call-update
  46.7 0.0 copy-done.1
  46.7 0.0 copy-done.2
  46.8 4.4 %all_gather.10 = bf16[2048,4]{0,1:T(4,128)(2,1)S(1)} all-gather(bf16[1024,4]{0,1:T(4,128)(2,1)S(1)} %multiply_convert_fusion), channel_id=1, replica_groups=mesh['bank'=16,'zero'=2] {'zero'}, dimensions={0}, use_global_device_ids=true | all-gather | bytes 24576 | tf_op jit(solution)/shard_map/all_gather | solution.py:14
  51.1 22.2 %all-gather = bf16[16,4,2048]{2,1,0:T(4,128)(2,1)S(1)} all-gather(bf16[1,4,2048]{2,1,0:T(4,128)(2,1)S(1)} %bitcast.5), channel_id=1, replica_groups=mesh['bank'=16,'zero'=2] {'bank'}, dimensions={0}, use_global_device_ids=true | all-gather | bytes 278528 | tf_op jit(solution)/shard_map/all_gather | solution.py:15
  73.3 0.8 reshape.9
  74.1 243.3 %all-gather.3.cloned.1.call-done = bf16[4,1408,2048]{2,1,0:T(8,128)(2,1)} async-done(((bf16[4,1408,1024]{2,1,0:T(8,128)(2,1)}), bf16[4,1408,2048]{2,1,0:T(8,128)(2,1)}) %all-gather.3.cloned.1.call-update) | async-done | bytes 23068688 | tf_op jit(solution)/shard_map/all_gather | solution.py:12
  317.4 20.3 %copy.8 = bf16[4,1408,2048]{2,1,0:T(8,128)(2,1)} copy(bf16[4,1408,2048]{2,1,0:T(8,128)(2,1)} %all-gather.3.cloned.1.call-done) | data formatting | bytes 46137344
  (2 shorter events, 0.0 us)
Async XLA Ops:
  7.2 310.3 %all-gather.3.cloned.1.call-start = ((), (), s32[]{:S(2)}) async-start(), calls=%async_computation | async-start | bytes 34603008 | tf_op jit(solution)/shard_map/all_gather | solution.py:12
  29.7 17.0 %copy-start = (f32[4,1408]{1,0:T(4,128)}, f32[4,1408]{1,0:T(4,128)S(1)}, u32[]{:S(2)}) copy-start(f32[4,1408]{1,0:T(4,128)S(1)} %sqrt.3) | copy-start | bytes 67588
  29.7 17.0 %copy-start.1 = (f32[1024,4]{0,1:T(4,128)S(1)}, f32[1024,4]{0,1:T(4,128)}, u32[]{:S(2)}) copy-start(f32[1024,4]{0,1:T(4,128)} %param.6) | copy-start | bytes 49156
  29.7 17.0 %copy-start.2 = (f32[1024]{0:T(1024)S(1)}, f32[1024]{0:T(1024)}, u32[]{:S(2)}) copy-start(f32[1024]{0:T(1024)} %param.7) | copy-start | bytes 12292
Sparse Core Ops, SparseCore 0:
  46.9 270.5 all-gather.2
where the time goes:
time: 345 us
  waiting for transfers between devices  243 us (70%)
  blocking collectives  36.4 us (11%)
  other arithmetic  29.5 us (9%)
  local copies, waits for them, and re-layouts  21.1 us (6%)
  between operations  14.1 us (4%)
    all_gather x1, waiting for transfers between devices, body(): final_down = lax.all_gather(narrow_down, 'zero', axis=2, tiled=True)  243 us
    all_gather x1, blocking collectives, body(): serve_router = lax.all_gather(row_router, 'bank', axis=1, tiled=True)  22.2 us
    unnamed x8, local copies, waits for them, and re-layouts  21.1 us
    convert_element_type x1, other arithmetic, body(): (merged_down / jnp.expand_dims(scale_down, 2)).astype(jnp.bfloat16)  17 us
    reduce_sum x1, other arithmetic, body(): total_down = lax.psum(jnp.sum(merged_down * merged_down, axis=2), 'zero')  12.6 us
    psum x1, blocking collectives, body(): total_down = lax.psum(jnp.sum(merged_down * merged_down, axis=2), 'zero')  9.91 us
  transfers between devices with their start and end apart: 1, of which 1 were waited for; matrix products, arithmetic and copies ran while one was open for 0% of the time, Pallas kernels for 0%

commit v1 on v0

--- a/solution.py
+++ b/solution.py
@@ -1,10 +1,181 @@
+import functools
+
 import jax
 import jax.numpy as jnp
 from jax import lax
+from jax.experimental import pallas as pl
+from jax.experimental.pallas import tpu as pltpu
 from jax.sharding import PartitionSpec as P
 
 
-def body(master_down, second_down, router_weight, router_gain):
+LANES = 128
+PAIR = ((0, 1), (1, 0))
+
+
+def cost(us):
+    return pl.CostEstimate(flops=int(us * 1e6), bytes_accessed=1024, transcendentals=0)
+
+
+def params():
+    return pltpu.CompilerParams(vmem_limit_bytes=16 * 1024 * 1024)
+
+
+def tile(m_ref, s_ref, b, k):
+    rows, cols = pl.ds(b * LANES, LANES), pl.ds(k * LANES, LANES)
+    return m_ref[rows, cols] + s_ref[rows, cols].astype(jnp.float32)
+
+
+def sums_kernel(m_ref, s_ref, *refs):
+    sums_ref = refs[-1]
+    for b in range(m_ref.shape[0] // LANES):
+        acc = jnp.zeros((LANES, LANES), jnp.float32)
+        for k in range(m_ref.shape[1] // LANES):
+            v = tile(m_ref, s_ref, b, k)
+            acc = acc + v * v
+        sums_ref[b] = jnp.sum(acc.T, axis=0, keepdims=True)
+
+
+def norm_kernel(m_ref, s_ref, own_ref, other_ref, *refs):
+    send_ref, out_ref = refs[-2:]
+    for b in range(m_ref.shape[0] // LANES):
+        inverse = 1.0 / jnp.sqrt(own_ref[b] + other_ref[b])
+        inverse = jnp.broadcast_to(inverse, (LANES, LANES)).T
+        rows = pl.ds(b * LANES, LANES)
+        for k in range(m_ref.shape[1] // LANES):
+            cols = pl.ds(k * LANES, LANES)
+            r = (tile(m_ref, s_ref, b, k) * inverse).astype(jnp.bfloat16)
+            send_ref[rows, cols] = r
+            out_ref[rows, cols] = r
+
+
+def place_kernel(row, recv_ref, _, out_ref, sem):
+    rows, width = recv_ref.shape
+    side = pl.multiple_of((1 - lax.axis_index("zero")) * width, LANES)
+    copy = pltpu.make_async_copy(recv_ref, out_ref.at[pl.ds(row, rows), pl.ds(side, width)], sem)
+    copy.start()
+    copy.wait()
+
+
+def step_rows(first, count):
+    for rows in (512, 256):
+        if first % rows == 0 and count % rows == 0:
+            return rows
+    return LANES
+
+
+def in_hbm(x):
+    return pltpu.with_memory_space_constraint(x, pltpu.HBM)
+
+
+def sums_of(m, s, first, count, after=None):
+    rows, width = step_rows(first, count), m.shape[1]
+    at = first // rows
+    block = pl.BlockSpec((rows, width), lambda i: (at + i, 0))
+    held = [] if after is None else [after]
+    return pl.pallas_call(
+        sums_kernel,
+        grid=(count // rows,),
+        in_specs=[block, block] + [pl.BlockSpec(memory_space=pl.ANY)] * len(held),
+        out_specs=pl.BlockSpec((rows // LANES, 1, LANES), lambda i: (i, 0, 0)),
+        out_shape=jax.ShapeDtypeStruct((count // LANES, 1, LANES), jnp.float32),
+        compiler_params=params(),
+        cost_estimate=cost(count * 0.002),
+        name="sums",
+    )(m, s, *held)
+
+
+def norm_of(m, s, own, other, base, first, count, out):
+    rows, width = min(step_rows(first, count), step_rows(first - base, count)), m.shape[1]
+    at, near = first // rows, (first - base) // rows
+    block = pl.BlockSpec((rows, width), lambda i: (at + i, 0))
+    sums = pl.BlockSpec((rows // LANES, 1, LANES), lambda i: (near + i, 0, 0))
+    whole = jax.ShapeDtypeStruct((m.shape[0], 2 * width), jnp.bfloat16)
+    held = [] if out is None else [out]
+    return pl.pallas_call(
+        norm_kernel,
+        grid=(count // rows,),
+        in_specs=[block, block, sums, sums] + [pl.BlockSpec(memory_space=pl.ANY)] * len(held),
+        out_specs=[
+            pl.BlockSpec((rows, width), lambda i: (i, 0)),
+            pl.BlockSpec((rows, width), lambda i: (at + i, lax.axis_index("zero"))),
+        ],
+        out_shape=[jax.ShapeDtypeStruct((count, width), jnp.bfloat16), whole],
+        input_output_aliases={4: 1} if held else {},
+        compiler_params=params(),
+        cost_estimate=cost(count * 0.003),
+        name="norm",
+    )(m, s, own, other, *held)
+
+
+def place(recv, out, row):
+    return pl.pallas_call(
+        functools.partial(place_kernel, row),
+        in_specs=[pl.BlockSpec(memory_space=pltpu.VMEM), pl.BlockSpec(memory_space=pl.ANY)],
+        out_specs=pl.BlockSpec(memory_space=pl.ANY),
+        out_shape=jax.ShapeDtypeStruct(out.shape, out.dtype),
+        scratch_shapes=[pltpu.SemaphoreType.DMA],
+        input_output_aliases={1: 0},
+        compiler_params=params(),
+        cost_estimate=cost(1),
+        name="place",
+    )(recv, out)
+
+
+def swap(x):
+    return lax.ppermute(x, "zero", PAIR)
+
+
+def cuts(blocks):
+    sizes = [2]
+    blocks -= 2
+    while blocks > 8:
+        sizes.append(8)
+        blocks -= 8
+    while blocks > 1:
+        sizes.append(blocks // 2)
+        blocks -= blocks // 2
+    return sizes + [1]
+
+
+HEAD = (3, 1)
+
+
+def pair_body(master_down, second_down, router_weight, router_gain):
+    return pair_steps(master_down, second_down, router_weight, router_gain)
+
+
+def pair_steps(master_down, second_down, router_weight, router_gain):
+    experts, inner, width = master_down.shape
+    n = experts * inner
+    m, s = in_hbm(master_down.reshape(n, width)), in_hbm(second_down.reshape(n, width))
+    head = sum(HEAD) * LANES
+
+    own0 = sums_of(m, s, 0, head)
+    other0 = swap(own0)
+    row, out, recvs = 0, None, []
+    for i, size in enumerate((*HEAD, *cuts((n - head) // LANES))):
+        late = row >= head
+        send, out = norm_of(m, s, *((own1, other1, head) if late else (own0, other0, 0)), row, size * LANES, out)
+        recvs.append((row, swap(send)))
+        row += size * LANES
+        if i == 0:
+            own1 = sums_of(m, s, head, n - head, send)
+            other1 = swap(own1)
+
+    part_router = (router_weight * router_gain[:, None]).astype(jnp.bfloat16)
+    me = lax.axis_index("zero")
+    other_router = swap(part_router)
+    low, high = jnp.where(me == 0, part_router, other_router), jnp.where(me == 0, other_router, part_router)
+    serve_router = lax.all_gather(jnp.concatenate([low, high], 0), "bank", axis=1, tiled=True)
+
+    for row, recv in recvs:
+        out = place(recv, out, row)
+    total = jnp.concatenate([own0 + other0, own1 + other1], 0)
+    scale_down = jnp.sqrt(total).reshape(experts, inner)
+    return out.reshape(experts, inner, 2 * width), scale_down, serve_router
+
+
+def gather_body(master_down, second_down, router_weight, router_gain):
     merged_down = master_down + second_down.astype(jnp.float32)
     total_down = lax.psum(jnp.sum(merged_down * merged_down, axis=2), "zero")
     scale_down = jnp.sqrt(total_down)
@@ -17,8 +188,9 @@
 
 
 def solution(mesh):
+    pair = mesh.shape["zero"] == 2
     return jax.shard_map(
-        body,
+        pair_body if pair else gather_body,
         mesh=mesh,
         in_specs=(P("bank", None, "zero"), P("bank", None, "zero"), P("zero", "bank"), P("zero")),
         out_specs=(P("bank", None, None), P("bank", None), P()),

time: 345 us -> 309 us (0.90)
  Pallas kernels: 0 us -> 72.7 us
  waiting for transfers between devices: 243 us -> 187 us
  other arithmetic: 29.5 us -> 0.16 us
  starting transfers between devices: 0.04 us -> 18.6 us
  local copies, waits for them, and re-layouts: 21.1 us -> 4.6 us
  between operations: 14.1 us -> 0.81 us
  blocking collectives: 36.4 us -> 23.8 us
    all_gather x1 -> x0, waiting for transfers between devices: 243 us -> none  [body(): final_down = lax.all_gather(narrow_down, 'zero', axis=2, tiled=True)]
    ppermute x0 -> x14, waiting for transfers between devices: none -> 187 us  [swap(): return lax.ppermute(x, 'zero', PAIR)]
    pallas_call x0 -> x24, Pallas kernels: none -> 72.7 us  [the longest x11 39.3 us: norm_of(): pl.pallas_call(norm_kernel, grid=(count // rows,), in_specs=[block, block...]
    ppermute x0 -> x14, starting transfers between devices: none -> 18.6 us  [swap(): return lax.ppermute(x, 'zero', PAIR)]
    unnamed x8 -> x13, local copies, waits for them, and re-layouts: 21.1 us -> 3.98 us
    convert_element_type x2 -> x1, other arithmetic: 17 us -> 0.01 us  [pair_steps(): part_router = (router_weight * router_gain[:, None]).astype(jnp.bfloat16)]
    reduce_sum x1 -> x0, other arithmetic: 12.6 us -> none  [body(): total_down = lax.psum(jnp.sum(merged_down * merged_down, axis=2), 'zero')]
    psum x1 -> x0, blocking collectives: 9.91 us -> none  [body(): total_down = lax.psum(jnp.sum(merged_down * merged_down, axis=2), 'zero')]
  transfers between devices with their start and end apart: 1 -> 14, of which waited for: 1 -> 4; matrix products, arithmetic and copies ran while one was open for 0% -> 1% of each run, Pallas kernels for 0% -> 15%
where the time goes in v1:
time: 309 us; the launch traced here: 308 us
  waiting for transfers between devices  187 us (61%)
  Pallas kernels  72.7 us (24%)
  blocking collectives  23.8 us (8%)
  starting transfers between devices  18.6 us (6%)
  local copies, waits for them, and re-layouts  4.6 us (1%)
    ppermute x14, waiting for transfers between devices, swap(): return lax.ppermute(x, 'zero', PAIR)  187 us
    pallas_call x11, Pallas kernels, norm_of(): pl.pallas_call(norm_kernel, grid=(count // rows,), in_specs=[block, block...  39.3 us
    all_gather x1, blocking collectives, pair_steps(): lax.all_gather(jnp.concatenate([low, high], 0), 'bank', axis=1, tiled=True)  23.8 us
    ppermute x14, starting transfers between devices, swap(): return lax.ppermute(x, 'zero', PAIR)  18.6 us
    pallas_call x11, Pallas kernels, place(): pl.pallas_call(functools.partial(place_kernel, row), in_specs=[pl.BlockSp...  18.4 us
    pallas_call x2, Pallas kernels, sums_of(): pl.pallas_call(sums_kernel, grid=(count // rows,), in_specs=[block, block...  14.9 us
  transfers between devices with their start and end apart: 14, of which 4 were waited for; matrix products, arithmetic and copies ran while one was open for 1% of the time, Pallas kernels for 15%

profile of v1, /device:TPU:0, one launch (start us, length us, event | category | flops | bytes accessed | tf_op | source)
XLA Modules:
  0.0 307.8 jit_solution(3242945605904131761)
XLA Ops:
  0.6 2.2 sums.2.own_ref
  2.8 3.1 collective-permute-start
  5.9 1.6 collective-permute-done.other_ref
  7.5 3.5 %norm.11 = (bf16[384,1024]{1,0:T(8,128)(2,1)S(1)}, bf16[5632,2048]{1,0:T(8,128)(2,1)}) custom-call(f32[5632,1024]{1,0:T(8,128)} %bitcast.10, bf16[5632,1024]{1,0:T(8,128)(2,1)} %bitcast.23, f32[4,1,128]{2,1,0:T(1,128)S(1)} %sums.2.own_ref, f32[4,1,128]{2,1,0:T(1,128)S(1)} %collective-permute-done.other_ref), custom_call_target="tpu_custom_call" | custom-call | flops 1152000 | bytes 1024 | tf_op jit(solution)/shard_map/norm/pallas_call | solution.py:94
  10.9 12.7 %sums.3.own_ref = f32[40,1,128]{2,1,0:T(1,128)S(1)} custom-call(f32[5632,1024]{1,0:T(8,128)} %bitcast.11, bf16[5632,1024]{1,0:T(8,128)(2,1)} %bitcast.24, bf16[384,1024]{1,0:T(8,128)(2,1)S(1)} %get-tuple-element.25.refs_0_), custom_call_target="tpu_custom_call" | custom-call | flops 10240000 | bytes 1024 | tf_op jit(solution)/shard_map/sums/pallas_call | solution.py:75
  23.7 2.1 collective-permute-start.1
  25.7 2.0 norm.12
  27.7 2.4 norm.13
  30.1 5.4 %norm.14 = (bf16[1024,1024]{1,0:T(8,128)(2,1)}, bf16[5632,2048]{1,0:T(8,128)(2,1)}) custom-call(f32[5632,1024]{1,0:T(8,128)} %bitcast.14, bf16[5632,1024]{1,0:T(8,128)(2,1)} %bitcast.27, f32[40,1,128]{2,1,0:T(1,128)S(1)} %sums.3.own_ref, f32[40,1,128]{2,1,0:T(1,128)S(1)} %collective-permute-done.1.other_ref, ...), custom_call_target="tpu_custom_call", output_to_operand_aliasing={{1}: (4, {})} | custom-call | flops 3072000 | bytes 1024 | tf_op jit(solution)/shard_map/norm/pallas_call | solution.py:94
  35.5 1.8 collective-permute-start.9
  37.3 5.4 %norm.15 = (bf16[1024,1024]{1,0:T(8,128)(2,1)}, bf16[5632,2048]{1,0:T(8,128)(2,1)}) custom-call(f32[5632,1024]{1,0:T(8,128)} %bitcast.15, bf16[5632,1024]{1,0:T(8,128)(2,1)} %bitcast.28, f32[40,1,128]{2,1,0:T(1,128)S(1)} %sums.3.own_ref, f32[40,1,128]{2,1,0:T(1,128)S(1)} %collective-permute-done.1.other_ref, ...), custom_call_target="tpu_custom_call", output_to_operand_aliasing={{1}: (4, {})} | custom-call | flops 3072000 | bytes 1024 | tf_op jit(solution)/shard_map/norm/pallas_call | solution.py:94
  42.9 5.4 %norm.16 = (bf16[1024,1024]{1,0:T(8,128)(2,1)}, bf16[5632,2048]{1,0:T(8,128)(2,1)}) custom-call(f32[5632,1024]{1,0:T(8,128)} %bitcast.16, bf16[5632,1024]{1,0:T(8,128)(2,1)} %bitcast.29, f32[40,1,128]{2,1,0:T(1,128)S(1)} %sums.3.own_ref, f32[40,1,128]{2,1,0:T(1,128)S(1)} %collective-permute-done.1.other_ref, ...), custom_call_target="tpu_custom_call", output_to_operand_aliasing={{1}: (4, {})} | custom-call | flops 3072000 | bytes 1024 | tf_op jit(solution)/shard_map/norm/pallas_call | solution.py:94
  48.4 1.8 collective-permute-start.7
  50.4 1.9 collective-permute-start.13
  52.3 5.4 %norm.17 = (bf16[1024,1024]{1,0:T(8,128)(2,1)}, bf16[5632,2048]{1,0:T(8,128)(2,1)}) custom-call(f32[5632,1024]{1,0:T(8,128)} %bitcast.17, bf16[5632,1024]{1,0:T(8,128)(2,1)} %bitcast.30, f32[40,1,128]{2,1,0:T(1,128)S(1)} %sums.3.own_ref, f32[40,1,128]{2,1,0:T(1,128)S(1)} %collective-permute-done.1.other_ref, ...), custom_call_target="tpu_custom_call", output_to_operand_aliasing={{1}: (4, {})} | custom-call | flops 3072000 | bytes 1024 | tf_op jit(solution)/shard_map/norm/pallas_call | solution.py:94
  57.7 119.6 %collective-permute-done.13 = bf16[1024,4]{0,1:T(4,128)(2,1)S(1)} collective-permute-done((bf16[1024,4]{0,1:T(4,128)(2,1)S(1)}, bf16[1024,4]{0,1:T(4,128)(2,1)S(1)}, u32[]{:S(2)}, u32[]{:S(2)}) %collective-permute-start.13) | collective-permute-done | bytes 8224 | tf_op jit(solution)/shard_map/ppermute | solution.py:125
  177.3 1.5 collective-permute-start.10
  179.4 12.8 %collective-permute-done.10.recv_ref = bf16[256,1024]{1,0:T(8,128)(2,1)S(1)} collective-permute-done((bf16[256,1024]{1,0:T(8,128)(2,1)S(1)}, bf16[256,1024]{1,0:T(8,128)(2,1)S(1)}, u32[]{:S(2)}, u32[]{:S(2)}) %collective-permute-start.10) | collective-permute-done | bytes 524320 | tf_op jit(solution)/shard_map/ppermute | solution.py:125
  192.1 1.5 collective-permute-start.12
  193.6 3.7 %norm.18 = (bf16[384,1024]{1,0:T(8,128)(2,1)}, bf16[5632,2048]{1,0:T(8,128)(2,1)}) custom-call(f32[5632,1024]{1,0:T(8,128)} %bitcast.18, bf16[5632,1024]{1,0:T(8,128)(2,1)} %bitcast.31, f32[40,1,128]{2,1,0:T(1,128)S(1)} %sums.3.own_ref, f32[40,1,128]{2,1,0:T(1,128)S(1)} %collective-permute-done.1.other_ref, ...), custom_call_target="tpu_custom_call", output_to_operand_aliasing={{1}: (4, {})} | custom-call | flops 1152000 | bytes 1024 | tf_op jit(solution)/shard_map/norm/pallas_call | solution.py:94
  197.3 53.2 %collective-permute-done.12.recv_ref = bf16[384,1024]{1,0:T(8,128)(2,1)S(1)} collective-permute-done((bf16[384,1024]{1,0:T(8,128)(2,1)S(1)}, bf16[384,1024]{1,0:T(8,128)(2,1)S(1)}, u32[]{:S(2)}, u32[]{:S(2)}) %collective-permute-start.12) | collective-permute-done | bytes 786464 | tf_op jit(solution)/shard_map/ppermute | solution.py:125
  252.4 2.1 norm.19
  254.4 2.1 norm.20
  256.5 2.1 norm.21
  261.7 23.8 %all-gather = bf16[16,4,2048]{2,1,0:T(4,128)(2,1)} all-gather(bf16[1,4,2048]{2,1,0:T(4,128)(2,1)S(1)} %maximum_bitcast_fusion), channel_id=1, replica_groups=mesh['bank'=16,'zero'=2] {'bank'}, dimensions={0}, use_global_device_ids=true | all-gather | bytes 278528 | tf_op jit(solution)/shard_map/all_gather | solution.py:169
  285.5 1.7 reshape.30
  293.1 2.9 place.15._
  296.0 2.9 place.16._
  298.9 2.9 place.17._
  302.8 1.7 place.19._
  304.5 1.7 place.20._
  306.1 1.7 place.21
  (41 shorter events, 12.8 us)
Async XLA Ops:
  2.8 4.6 %collective-permute-start = (f32[4,1,128]{2,1,0:T(1,128)S(1)}, f32[4,1,128]{2,1,0:T(1,128)S(1)}, u32[]{:S(2)}, u32[]{:S(2)}) collective-permute-start(f32[4,1,128]{2,1,0:T(1,128)S(1)} %sums.2.own_ref), channel_id=1, source_target_pairs={{0,1},{1,0},{2,3},{3,2},{4,5},{5,4},{6,7},{7,6},{8,9},{9,8},{10,11... | collective-permute-start | bytes 6152 | tf_op jit(solution)/shard_map/ppermute | solution.py:125
  23.7 4.1 %collective-permute-start.1 = (f32[40,1,128]{2,1,0:T(1,128)S(1)}, f32[40,1,128]{2,1,0:T(1,128)S(1)}, u32[]{:S(2)}, u32[]{:S(2)}) collective-permute-start(f32[40,1,128]{2,1,0:T(1,128)S(1)} %sums.3.own_ref), channel_id=1, source_target_pairs={{0,1},{1,0},{2,3},{3,2},{4,5},{5,4},{6,7},{7,6},{8,9},{9,8},{10,11... | collective-permute-start | bytes 61448 | tf_op jit(solution)/shard_map/ppermute | solution.py:125
  35.5 223.0 %collective-permute-start.9 = (bf16[1024,1024]{1,0:T(8,128)(2,1)}, bf16[1024,1024]{1,0:T(8,128)(2,1)S(1)}, u32[]{:S(2)}, u32[]{:S(2)}) collective-permute-start(bf16[1024,1024]{1,0:T(8,128)(2,1)} %get-tuple-element.43), channel_id=1, source_target_pairs={{0,1},{1,0},{2,3},{3,2},{4,5},{5,4},{6,7},{7,6},{8,9},{9,8},{10,11... | collective-permute-start | bytes 6291464 | tf_op jit(solution)/shard_map/ppermute | solution.py:125
  42.7 216.9 %collective-permute-start.8 = (bf16[1024,1024]{1,0:T(8,128)(2,1)}, bf16[1024,1024]{1,0:T(8,128)(2,1)}, u32[]{:S(2)}, u32[]{:S(2)}) collective-permute-start(bf16[1024,1024]{1,0:T(8,128)(2,1)} %get-tuple-element.42), channel_id=1, source_target_pairs={{0,1},{1,0},{2,3},{3,2},{4,5},{5,4},{6,7},{7,6},{8,9},{9,8},{10,11... | collective-permute-start | bytes 6291464 | tf_op jit(solution)/shard_map/ppermute | solution.py:125
  42.9 7.5 %copy-start.4 = (f32[1024,4]{0,1:T(4,128)S(1)}, f32[1024,4]{0,1:T(4,128)}, u32[]{:S(2)}) copy-start(f32[1024,4]{0,1:T(4,128)} %param.6) | copy-start | bytes 49156
  42.9 7.5 %copy-start.5 = (f32[1024]{0:T(1024)S(1)}, f32[1024]{0:T(1024)}, u32[]{:S(2)}) copy-start(f32[1024]{0:T(1024)} %param.7) | copy-start | bytes 12292
  48.4 212.2 %collective-permute-start.7 = (bf16[1024,1024]{1,0:T(8,128)(2,1)}, bf16[1024,1024]{1,0:T(8,128)(2,1)}, u32[]{:S(2)}, u32[]{:S(2)}) collective-permute-start(bf16[1024,1024]{1,0:T(8,128)(2,1)} %get-tuple-element.41), channel_id=1, source_target_pairs={{0,1},{1,0},{2,3},{3,2},{4,5},{5,4},{6,7},{7,6},{8,9},{9,8},{10,11... | collective-permute-start | bytes 6291464 | tf_op jit(solution)/shard_map/ppermute | solution.py:125
  50.2 128.6 %collective-permute-start.11 = (bf16[128,1024]{1,0:T(8,128)(2,1)S(1)}, bf16[128,1024]{1,0:T(8,128)(2,1)S(1)}, u32[]{:S(2)}, u32[]{:S(2)}) collective-permute-start(bf16[128,1024]{1,0:T(8,128)(2,1)S(1)} %get-tuple-element.45), channel_id=1, source_target_pairs={{0,1},{1,0},{2,3},{3,2},{4,5},{5,4},{6,7},{7,6},{8,9},{9,8},{10,11... | collective-permute-start | bytes 786440 | tf_op jit(solution)/shard_map/ppermute | solution.py:125
  50.4 126.9 %collective-permute-start.13 = (bf16[1024,4]{0,1:T(4,128)(2,1)S(1)}, bf16[1024,4]{0,1:T(4,128)(2,1)S(1)}, u32[]{:S(2)}, u32[]{:S(2)}) collective-permute-start(bf16[1024,4]{0,1:T(4,128)(2,1)S(1)} %multiply_convert_fusion), channel_id=1, source_target_pairs={{0,1},{1,0},{2,3},{3,2},{4,5},{5,4},{6,7},{7,6},{8,9},{9,8},{10,11... | collective-permute-start | bytes 24584 | tf_op jit(solution)/shard_map/ppermute | solution.py:125
  177.3 14.8 %collective-permute-start.10 = (bf16[256,1024]{1,0:T(8,128)(2,1)S(1)}, bf16[256,1024]{1,0:T(8,128)(2,1)S(1)}, u32[]{:S(2)}, u32[]{:S(2)}) collective-permute-start(bf16[256,1024]{1,0:T(8,128)(2,1)S(1)} %get-tuple-element.44), channel_id=1, source_target_pairs={{0,1},{1,0},{2,3},{3,2},{4,5},{5,4},{6,7},{7,6},{8,9},{9,8},{10,11... | collective-permute-start | bytes 1572872 | tf_op jit(solution)/shard_map/ppermute | solution.py:125
  178.8 18.5 %copy-start.2 = (bf16[128,1024]{1,0:T(8,128)(2,1)}, bf16[128,1024]{1,0:T(8,128)(2,1)S(1)}, u32[]{:S(2)}) copy-start(bf16[128,1024]{1,0:T(8,128)(2,1)S(1)} %collective-permute-done.11.recv_ref) | copy-start | bytes 786436
  178.8 120.1 %collective-permute-start.6 = (bf16[1024,1024]{1,0:T(8,128)(2,1)}, bf16[1024,1024]{1,0:T(8,128)(2,1)}, u32[]{:S(2)}, u32[]{:S(2)}) collective-permute-start(bf16[1024,1024]{1,0:T(8,128)(2,1)} %get-tuple-element.40), channel_id=1, source_target_pairs={{0,1},{1,0},{2,3},{3,2},{4,5},{5,4},{6,7},{7,6},{8,9},{9,8},{10,11... | collective-permute-start | bytes 6291464 | tf_op jit(solution)/shard_map/ppermute | solution.py:125
  192.1 58.4 %collective-permute-start.12 = (bf16[384,1024]{1,0:T(8,128)(2,1)S(1)}, bf16[384,1024]{1,0:T(8,128)(2,1)S(1)}, u32[]{:S(2)}, u32[]{:S(2)}) collective-permute-start(bf16[384,1024]{1,0:T(8,128)(2,1)S(1)} %get-tuple-element.25.refs_0_), channel_id=1, source_target_pairs={{0,1},{1,0},{2,3},{3,2},{4,5},{5,4},{6,7},{7,6},{8,9},{9,8},{10,11... | collective-permute-start | bytes 2359304 | tf_op jit(solution)/shard_map/ppermute | solution.py:125
  250.5 0.9 copy-start
  251.4 50.4 %collective-permute-start.5 = (bf16[384,1024]{1,0:T(8,128)(2,1)}, bf16[384,1024]{1,0:T(8,128)(2,1)S(1)}, u32[]{:S(2)}, u32[]{:S(2)}) collective-permute-start(bf16[384,1024]{1,0:T(8,128)(2,1)} %get-tuple-element.39), channel_id=1, source_target_pairs={{0,1},{1,0},{2,3},{3,2},{4,5},{5,4},{6,7},{7,6},{8,9},{9,8},{10,11... | collective-permute-start | bytes 2359304 | tf_op jit(solution)/shard_map/ppermute | solution.py:125
  258.5 44.3 %collective-permute-start.4 = (bf16[128,1024]{1,0:T(8,128)(2,1)}, bf16[128,1024]{1,0:T(8,128)(2,1)}, u32[]{:S(2)}, u32[]{:S(2)}) collective-permute-start(bf16[128,1024]{1,0:T(8,128)(2,1)} %get-tuple-element.38), channel_id=1, source_target_pairs={{0,1},{1,0},{2,3},{3,2},{4,5},{5,4},{6,7},{7,6},{8,9},{9,8},{10,11... | collective-permute-start | bytes 786440 | tf_op jit(solution)/shard_map/ppermute | solution.py:125
  259.6 44.8 %collective-permute-start.3 = (bf16[128,1024]{1,0:T(8,128)(2,1)}, bf16[128,1024]{1,0:T(8,128)(2,1)}, u32[]{:S(2)}, u32[]{:S(2)}) collective-permute-start(bf16[128,1024]{1,0:T(8,128)(2,1)} %get-tuple-element.37), channel_id=1, source_target_pairs={{0,1},{1,0},{2,3},{3,2},{4,5},{5,4},{6,7},{7,6},{8,9},{9,8},{10,11... | collective-permute-start | bytes 786440 | tf_op jit(solution)/shard_map/ppermute | solution.py:125
  260.5 45.6 %collective-permute-start.2 = (bf16[128,1024]{1,0:T(8,128)(2,1)}, bf16[128,1024]{1,0:T(8,128)(2,1)}, u32[]{:S(2)}, u32[]{:S(2)}) collective-permute-start(bf16[128,1024]{1,0:T(8,128)(2,1)} %get-tuple-element.36), channel_id=1, source_target_pairs={{0,1},{1,0},{2,3},{3,2},{4,5},{5,4},{6,7},{7,6},{8,9},{9,8},{10,11... | collective-permute-start | bytes 786440 | tf_op jit(solution)/shard_map/ppermute | solution.py:125
  287.9 1.1 copy-start.1
  289.1 1.1 copy-start.3

commit v2 on v1

v2 whole, which is shorter than its diff:
```python
import functools

import jax
import jax.numpy as jnp
from jax import lax
from jax.experimental import pallas as pl
from jax.experimental.pallas import tpu as pltpu
from jax.sharding import PartitionSpec as P


LANES = 128
PAIR = ((0, 1), (1, 0))
ANY = pl.BlockSpec(memory_space=pl.ANY)
VMEM = pl.BlockSpec(memory_space=pltpu.VMEM)
EARLY = 32
GROUPS = ((1,), (2, 1), (8, 4))
LEAST = 24


def cost(us):
    return pl.CostEstimate(flops=int(us * 1e6), bytes_accessed=1024, transcendentals=0)


def params():
    return pltpu.CompilerParams(vmem_limit_bytes=16 * 1024 * 1024)


def lane_tiles(ref):
    return [pl.ds(k * LANES, LANES) for k in range(ref.shape[-1] // LANES)]


def block_rows(b):
    return pl.ds(b * LANES, LANES)


def merged_tile(m_ref, s_ref, rows, cols):
    return m_ref[rows, cols] + s_ref[rows, cols].astype(jnp.float32)


def row_scales(own, other):
    inverse = 1.0 / jnp.sqrt(own + other)
    return jnp.broadcast_to(inverse, (LANES, LANES)).T


def head_kernel(first, early, m_hbm, s_hbm, *refs):
    sums_ref, merged_ref = refs[:2]
    m_ref, s_ref, sems = refs[-3:]
    blocks = merged_ref.shape[0] // LANES
    copies = []
    for b in range(blocks):
        there = pl.ds(first + b * LANES, LANES)
        copies.append(pltpu.make_async_copy(m_hbm.at[there], m_ref.at[block_rows(b)], sems.at[2 * b]))
        copies.append(pltpu.make_async_copy(s_hbm.at[there], s_ref.at[block_rows(b)], sems.at[2 * b + 1]))
    for copy in copies:
        copy.start()
    for b in range(blocks):
        copies[2 * b].wait()
        copies[2 * b + 1].wait()
        acc = jnp.zeros((LANES, LANES), jnp.float32)
        for cols in lane_tiles(m_ref):
            v = merged_tile(m_ref, s_ref, block_rows(b), cols)
            merged_ref[block_rows(b), cols] = v
            if early and b == 0:
                refs[2][:, cols] = v[:early]
            acc = acc + v * v
        sums_ref[b] = jnp.sum(acc.T, axis=0, keepdims=True)


def head_norm_kernel(first, merged_ref, own_ref, other_ref, *refs):
    send_ref = refs[-1]
    count, row = send_ref.shape[0], first
    while row < first + count:
        b, skip = row // LANES, row % LANES
        rows = min(LANES - skip, first + count - row)
        inverse = row_scales(own_ref[b], other_ref[b])[skip : skip + rows]
        for cols in lane_tiles(merged_ref):
            v = merged_ref[pl.ds(row, rows), cols] * inverse
            send_ref[pl.ds(row - first, rows), cols] = v.astype(jnp.bfloat16)
        row += rows


def sums_kernel(m_ref, s_ref, *refs):
    sums_ref = refs[-1]
    for b in range(m_ref.shape[0] // LANES):
        acc = jnp.zeros((LANES, LANES), jnp.float32)
        for cols in lane_tiles(m_ref):
            v = merged_tile(m_ref, s_ref, block_rows(b), cols)
            acc = acc + v * v
        sums_ref[b] = jnp.sum(acc.T, axis=0, keepdims=True)


def norm_kernel(m_ref, s_ref, own_ref, other_ref, *refs):
    send_ref, out_ref = refs[-2:]
    for b in range(m_ref.shape[0] // LANES):
        inverse = row_scales(own_ref[b], other_ref[b])
        for cols in lane_tiles(m_ref):
            r = (merged_tile(m_ref, s_ref, block_rows(b), cols) * inverse).astype(jnp.bfloat16)
            send_ref[block_rows(b), cols] = r
            out_ref[block_rows(b), cols] = r


def received_half(out_ref, row, shape):
    rows, width = shape
    side = pl.multiple_of((1 - lax.axis_index("zero")) * width, LANES)
    return out_ref.at[pl.ds(row, rows), pl.ds(side, width)]


def place_kernel(row, recv_ref, _, out_ref, sem):
    copy = pltpu.make_async_copy(recv_ref, received_half(out_ref, row, recv_ref.shape), sem)
    copy.start()
    copy.wait()


def place_early_kernel(recv_ref, own_ref, other_ref, _, out_ref, held_ref, sem):
    rows = recv_ref.shape[0]
    inverse = row_scales(own_ref[0], other_ref[0])[:rows]
    for cols in lane_tiles(recv_ref):
        held_ref[:, cols] = (recv_ref[:, cols] * inverse).astype(jnp.bfloat16)
    copy = pltpu.make_async_copy(held_ref, received_half(out_ref, 0, recv_ref.shape), sem)
    copy.start()
    copy.wait()


def in_hbm(x):
    return pltpu.with_memory_space_constraint(x, pltpu.HBM)


def in_vmem(x):
    return pltpu.with_memory_space_constraint(x, pltpu.VMEM)


def whole_of(m):
    return jax.ShapeDtypeStruct((m.shape[0], 2 * m.shape[1]), jnp.bfloat16)


def sums_shape(blocks):
    return jax.ShapeDtypeStruct((blocks, 1, LANES), jnp.float32)


def head_of(m, s, first, blocks, early, after=()):
    rows, width = blocks * LANES, m.shape[1]
    shapes = [sums_shape(blocks), jax.ShapeDtypeStruct((rows, width), jnp.float32)]
    shapes += [jax.ShapeDtypeStruct((early, width), jnp.float32)] if early else []
    return pl.pallas_call(
        functools.partial(head_kernel, first, early) if not after else after_of(functools.partial(head_kernel, first, early), 2, len(after)),
        in_specs=[ANY, ANY] + [ANY] * len(after),
        out_specs=[VMEM] * len(shapes),
        out_shape=shapes,
        scratch_shapes=[
            pltpu.VMEM((rows, width), m.dtype),
            pltpu.VMEM((rows, width), s.dtype),
            pltpu.SemaphoreType.DMA((2 * blocks,)),
        ],
        compiler_params=params(),
        cost_estimate=cost(1),
        name="head",
    )(m, s, *after)


def after_of(kernel, at, count):
    def held(*refs):
        return kernel(*refs[:at], *refs[at + count :])

    return held


def head_norm_of(merged, own, other, first, count):
    return pl.pallas_call(
        functools.partial(head_norm_kernel, first),
        in_specs=[VMEM] * 3,
        out_specs=VMEM,
        out_shape=jax.ShapeDtypeStruct((count, merged.shape[1]), jnp.bfloat16),
        compiler_params=params(),
        cost_estimate=cost(1),
        name="head_norm",
    )(merged, own, other)


def step_rows(*counts):
    for rows in (512, 256):
        if all(count % rows == 0 for count in counts):
            return rows
    return LANES


def sums_of(m, s, first, count, after):
    rows, width = step_rows(first, count), m.shape[1]
    at = first // rows
    block = pl.BlockSpec((rows, width), lambda i: (at + i, 0))
    return pl.pallas_call(
        after_of(sums_kernel, 2, 1),
        grid=(count // rows,),
        in_specs=[block, block, ANY],
        out_specs=pl.BlockSpec((rows // LANES, 1, LANES), lambda i: (i, 0, 0)),
        out_shape=sums_shape(count // LANES),
        compiler_params=params(),
        cost_estimate=cost(count * 0.002),
        name="sums",
    )(m, s, after)


def norm_of(m, s, own, other, base, first, count, out):
    rows, width = step_rows(first, first - base, count), m.shape[1]
    at, near = first // rows, (first - base) // rows
    block = pl.BlockSpec((rows, width), lambda i: (at + i, 0))
    sums = pl.BlockSpec((rows // LANES, 1, LANES), lambda i: (near + i, 0, 0))
    held = [] if out is None else [out]
    return pl.pallas_call(
        norm_kernel,
        grid=(count // rows,),
        in_specs=[block, block, sums, sums] + [ANY] * len(held),
        out_specs=[
            pl.BlockSpec((rows, width), lambda i: (i, 0)),
            pl.BlockSpec((rows, width), lambda i: (at + i, lax.axis_index("zero"))),
        ],
        out_shape=[jax.ShapeDtypeStruct((count, width), jnp.bfloat16), whole_of(m)],
        input_output_aliases={4: 1} if held else {},
        compiler_params=params(),
        cost_estimate=cost(count * 0.003),
        name="norm",
    )(m, s, own, other, *held)


def place(recv, out, row):
    return pl.pallas_call(
        functools.partial(place_kernel, row),
        in_specs=[VMEM, ANY],
        out_specs=ANY,
        out_shape=jax.ShapeDtypeStruct(out.shape, out.dtype),
        scratch_shapes=[pltpu.SemaphoreType.DMA],
        input_output_aliases={1: 0},
        compiler_params=params(),
        cost_estimate=cost(1),
        name="place",
    )(recv, out)


def place_early(recv, own, other, out):
    return pl.pallas_call(
        place_early_kernel,
        in_specs=[VMEM, VMEM, VMEM, ANY],
        out_specs=ANY,
        out_shape=jax.ShapeDtypeStruct(out.shape, out.dtype),
        scratch_shapes=[pltpu.VMEM(recv.shape, jnp.bfloat16), pltpu.SemaphoreType.DMA],
        input_output_aliases={3: 0},
        compiler_params=params(),
        cost_estimate=cost(1),
        name="place_early",
    )(recv, own, other, out)


def swap(x):
    return lax.ppermute(x, "zero", PAIR)


def last_cuts(blocks):
    sizes = []
    while blocks > 12:
        sizes.append(8)
        blocks -= 8
    while blocks > 1:
        sizes.append(blocks // 2)
        blocks -= blocks // 2
    return (*sizes, 1)


def plan(blocks):
    return (*GROUPS, last_cuts(blocks - sum(map(sum, GROUPS))))


def pair_steps(master_down, second_down, router_weight, router_gain):
    experts, inner, width = master_down.shape
    n = experts * inner
    m, s = in_hbm(master_down.reshape(n, width)), in_hbm(second_down.reshape(n, width))
    groups = plan(n // LANES)

    own0, merged0, early = head_of(m, s, 0, 1, EARLY)
    sums = [(own0, swap(own0))]
    other_early = swap(early)
    own1, merged1 = head_of(m, s, LANES, sum(groups[1]), 0, (early,))
    sums.append((own1, swap(own1)))
    heads = (merged0, merged1)

    out, recvs, row, i = None, [], 0, 0
    for g, chunks in enumerate(groups):
        base = row
        for c, size in enumerate(chunks):
            count = size * LANES
            if g < 2:
                skip = EARLY if row == 0 else 0
                send = head_norm_of(heads[g], *sums[g], row - base + skip, count - skip)
            else:
                skip = 0
                send, out = norm_of(m, s, *sums[g], base, row, count, out)
            if row + count < n:
                recvs.append((row + skip, swap(send)))
            else:
                half = count // 2
                recvs.append((row, swap(send[:half])))
                recvs.append((row + half, swap(send[half:])))
            row += count
            if g + 1 == len(sums) and g + 1 < len(groups) and c + 1 == max(1, len(chunks) - 1):
                first, rest = base + sum(chunks) * LANES, sum(groups[g + 1]) * LANES
                own = sums_of(m, s, first, rest, send)
                sums.append((own, swap(own)))
            i += 1

    _, out = norm_of(m, s, *sums[0], 0, 0, LANES, out)
    _, out = norm_of(m, s, *sums[1], LANES, LANES, sum(groups[1]) * LANES, out)

    part_router = (router_weight * router_gain[:, None]).astype(jnp.bfloat16)
    me = lax.axis_index("zero")
    other_router = swap(part_router)
    low, high = jnp.where(me == 0, part_router, other_router), jnp.where(me == 0, other_router, part_router)
    serve_router = lax.all_gather(jnp.concatenate([low, high], 0), "bank", axis=1, tiled=True)

    out = place_early(other_early, *sums[0], out)
    for row, recv in recvs[:-1]:
        out = place(recv, out, row)
    row, recv = recvs[-1]
    out = place(in_vmem(recv), out, row)
    total = jnp.concatenate([own + other for own, other in sums], 0)
    scale_down = jnp.sqrt(total).reshape(experts, inner)
    return out.reshape(experts, inner, 2 * width), scale_down, serve_router


def gather_body(master_down, second_down, router_weight, router_gain):
    merged_down = master_down + second_down.astype(jnp.float32)
    total_down = lax.psum(jnp.sum(merged_down * merged_down, axis=2), "zero")
    scale_down = jnp.sqrt(total_down)
    narrow_down = (merged_down / jnp.expand_dims(scale_down, 2)).astype(jnp.bfloat16)
    final_down = lax.all_gather(narrow_down, "zero", axis=2, tiled=True)
    part_router = (router_weight * router_gain[:, None]).astype(jnp.bfloat16)
    row_router = lax.all_gather(part_router, "zero", axis=0, tiled=True)
    serve_router = lax.all_gather(row_router, "bank", axis=1, tiled=True)
    return (final_down, scale_down, serve_router)


def solution(mesh):
    specs = dict(
        mesh=mesh,
        in_specs=(P("bank", None, "zero"), P("bank", None, "zero"), P("zero", "bank"), P("zero")),
        out_specs=(P("bank", None, None), P("bank", None), P()),
        check_vma=False,
    )
    general = jax.shard_map(gather_body, **specs)

    def step(master_down, *rest):
        experts, inner, width = master_down.shape
        blocks, over = divmod(experts // mesh.shape["bank"] * inner, LANES)
        if mesh.shape["zero"] != 2 or over or blocks < LEAST or width % (2 * LANES):
            return general(master_down, *rest)
        return jax.shard_map(pair_steps, **specs)(master_down, *rest)

    return step
```

time: 309 us -> 318 us (1.029)
  Pallas kernels: 72.7 us -> 77.1 us
  starting transfers between devices: 18.6 us -> 22.3 us
    pallas_call x13 -> x21, Pallas kernels: 33.3 us -> 39.5 us  [the longest x13 21.4 us: place(): pl.pallas_call(functools.partial(place_kernel, row), in_specs=[VMEM, ANY]...]
    ppermute x14 -> x19, starting transfers between devices: 18.6 us -> 22.3 us  [swap(): return lax.ppermute(x, 'zero', PAIR)]
    ppermute x14 -> x19, waiting for transfers between devices: 187 us -> 188 us  [swap(): return lax.ppermute(x, 'zero', PAIR)]
  transfers between devices with their start and end apart: 14 -> 19, of which waited for: 4 -> 4; matrix products, arithmetic and copies ran while one was open for 1% -> 1% of each run, Pallas kernels for 15% -> 21%
where the time goes in v2:
time: 318 us; the launch traced here: 317 us
  waiting for transfers between devices  188 us (59%)
  Pallas kernels  77.1 us (24%)
  blocking collectives  23.9 us (8%)
  starting transfers between devices  22.3 us (7%)
  local copies, waits for them, and re-layouts  4.49 us (1%)
    ppermute x19, waiting for transfers between devices, swap(): return lax.ppermute(x, 'zero', PAIR)  188 us
    pallas_call x11, Pallas kernels, norm_of(): pl.pallas_call(norm_kernel, grid=(count // rows,), in_specs=[block, block...  37.6 us
    all_gather x1, blocking collectives, pair_steps(): lax.all_gather(jnp.concatenate([low, high], 0), 'bank', axis=1, tiled=True)  23.9 us
    ppermute x19, starting transfers between devices, swap(): return lax.ppermute(x, 'zero', PAIR)  22.3 us
    pallas_call x13, Pallas kernels, place(): pl.pallas_call(functools.partial(place_kernel, row), in_specs=[VMEM, ANY]...  21.4 us
    pallas_call x2, Pallas kernels, sums_of(): pl.pallas_call(after_of(sums_kernel, 2, 1), grid=(count // rows,), in_spe...  13.9 us
  transfers between devices with their start and end apart: 19, of which 4 were waited for; matrix products, arithmetic and copies ran while one was open for 1% of the time, Pallas kernels for 21%

profile of v2, /device:TPU:0, one launch (start us, length us, event | category | flops | bytes accessed | tf_op | source)
XLA Modules:
  0.0 317.0 jit_solution(15127675505807446285)
XLA Ops:
  1.9 1.8 head.3
  3.7 3.1 collective-permute-start
  8.5 4.6 %sums.2.own_ref = f32[12,1,128]{2,1,0:T(1,128)S(1)} custom-call(f32[5632,1024]{1,0:T(8,128)} %bitcast.11, bf16[5632,1024]{1,0:T(8,128)(2,1)} %bitcast.26, bf16[256,1024]{1,0:T(8,128)(2,1)S(1)} %head_norm.3.refs_2_), custom_call_target="tpu_custom_call" | custom-call | flops 3072000 | bytes 1024 | tf_op jit(solution)/shard_map/sums/pallas_call | solution.py:190
  13.1 2.1 collective-permute-start.1
  15.3 1.9 collective-permute-start.17
  17.2 4.5 %norm.11 = (bf16[1024,1024]{1,0:T(8,128)(2,1)}, bf16[5632,2048]{1,0:T(8,128)(2,1)}) custom-call(f32[5632,1024]{1,0:T(8,128)} %bitcast.12, bf16[5632,1024]{1,0:T(8,128)(2,1)} %bitcast.27, f32[12,1,128]{2,1,0:T(1,128)S(1)} %sums.2.own_ref, f32[12,1,128]{2,1,0:T(1,128)S(1)} %collective-permute-done.1.other_ref), custom_call_target="tpu_custom_call" | custom-call | flops 3072000 | bytes 1024 | tf_op jit(solution)/shard_map/norm/pallas_call | solution.py:208
  21.7 1.7 collective-permute-start.12
  24.0 1.7 collective-permute-start.14
  25.6 9.3 %sums.3.own_ref = f32[28,1,128]{2,1,0:T(1,128)S(1)} custom-call(f32[5632,1024]{1,0:T(8,128)} %bitcast.13, bf16[5632,1024]{1,0:T(8,128)(2,1)} %bitcast.28, bf16[1024,1024]{1,0:T(8,128)(2,1)} %get-tuple-element.31.refs_2_), custom_call_target="tpu_custom_call" | custom-call | flops 7168000 | bytes 1024 | tf_op jit(solution)/shard_map/sums/pallas_call | solution.py:190
  35.4 47.8 %collective-permute-done.2.other_ref = f32[28,1,128]{2,1,0:T(1,128)S(1)} collective-permute-done((f32[28,1,128]{2,1,0:T(1,128)S(1)}, f32[28,1,128]{2,1,0:T(1,128)S(1)}, u32[]{:S(2)}, u32[]{:S(2)}) %collective-permute-start.2) | collective-permute-done | bytes 14368 | tf_op jit(solution)/shard_map/ppermute | solution.py:253
  84.5 3.5 %norm.12 = (bf16[512,1024]{1,0:T(8,128)(2,1)}, bf16[5632,2048]{1,0:T(8,128)(2,1)}) custom-call(f32[5632,1024]{1,0:T(8,128)} %bitcast.14, bf16[5632,1024]{1,0:T(8,128)(2,1)} %bitcast.29, f32[12,1,128]{2,1,0:T(1,128)S(1)} %sums.2.own_ref, f32[12,1,128]{2,1,0:T(1,128)S(1)} %collective-permute-done.1.other_ref, ...), custom_call_target="tpu_custom_call", output_to_operand_aliasing={{1}: (4, {})} | custom-call | flops 1536000 | bytes 1024 | tf_op jit(solution)/shard_map/norm/pallas_call | solution.py:208
  88.0 4.5 %norm.13 = (bf16[1024,1024]{1,0:T(8,128)(2,1)}, bf16[5632,2048]{1,0:T(8,128)(2,1)}) custom-call(f32[5632,1024]{1,0:T(8,128)} %bitcast.15, bf16[5632,1024]{1,0:T(8,128)(2,1)} %bitcast.30, f32[28,1,128]{2,1,0:T(1,128)S(1)} %sums.3.own_ref, f32[28,1,128]{2,1,0:T(1,128)S(1)} %collective-permute-done.2.other_ref, ...), custom_call_target="tpu_custom_call", output_to_operand_aliasing={{1}: (4, {})} | custom-call | flops 3072000 | bytes 1024 | tf_op jit(solution)/shard_map/norm/pallas_call | solution.py:208
  92.5 4.5 %norm.14 = (bf16[1024,1024]{1,0:T(8,128)(2,1)}, bf16[5632,2048]{1,0:T(8,128)(2,1)}) custom-call(f32[5632,1024]{1,0:T(8,128)} %bitcast.16, bf16[5632,1024]{1,0:T(8,128)(2,1)} %bitcast.31, f32[28,1,128]{2,1,0:T(1,128)S(1)} %sums.3.own_ref, f32[28,1,128]{2,1,0:T(1,128)S(1)} %collective-permute-done.2.other_ref, ...), custom_call_target="tpu_custom_call", output_to_operand_aliasing={{1}: (4, {})} | custom-call | flops 3072000 | bytes 1024 | tf_op jit(solution)/shard_map/norm/pallas_call | solution.py:208
  100.0 5.0 %norm.15 = (bf16[768,1024]{1,0:T(8,128)(2,1)}, bf16[5632,2048]{1,0:T(8,128)(2,1)}) custom-call(f32[5632,1024]{1,0:T(8,128)} %bitcast.17, bf16[5632,1024]{1,0:T(8,128)(2,1)} %bitcast.32, f32[28,1,128]{2,1,0:T(1,128)S(1)} %sums.3.own_ref, f32[28,1,128]{2,1,0:T(1,128)S(1)} %collective-permute-done.2.other_ref, ...), custom_call_target="tpu_custom_call", output_to_operand_aliasing={{1}: (4, {})} | custom-call | flops 2304000 | bytes 1024 | tf_op jit(solution)/shard_map/norm/pallas_call | solution.py:208
  105.0 88.3 %collective-permute-done.13.recv_ref = bf16[128,1024]{1,0:T(8,128)(2,1)S(1)} collective-permute-done((bf16[128,1024]{1,0:T(8,128)(2,1)S(1)}, bf16[128,1024]{1,0:T(8,128)(2,1)S(1)}, u32[]{:S(2)}, u32[]{:S(2)}) %collective-permute-start.13) | collective-permute-done | bytes 262176 | tf_op jit(solution)/shard_map/ppermute | solution.py:253
  196.1 3.8 %norm.16 = (bf16[384,1024]{1,0:T(8,128)(2,1)}, bf16[5632,2048]{1,0:T(8,128)(2,1)}) custom-call(f32[5632,1024]{1,0:T(8,128)} %bitcast.18, bf16[5632,1024]{1,0:T(8,128)(2,1)} %bitcast.33, f32[28,1,128]{2,1,0:T(1,128)S(1)} %sums.3.own_ref, f32[28,1,128]{2,1,0:T(1,128)S(1)} %collective-permute-done.2.other_ref, ...), custom_call_target="tpu_custom_call", output_to_operand_aliasing={{1}: (4, {})} | custom-call | flops 1152000 | bytes 1024 | tf_op jit(solution)/shard_map/norm/pallas_call | solution.py:208
  199.8 50.4 %collective-permute-done.11.recv_ref = bf16[512,1024]{1,0:T(8,128)(2,1)S(1)} collective-permute-done((bf16[512,1024]{1,0:T(8,128)(2,1)}, bf16[512,1024]{1,0:T(8,128)(2,1)S(1)}, u32[]{:S(2)}, u32[]{:S(2)}) %collective-permute-start.11) | collective-permute-done | bytes 1048608 | tf_op jit(solution)/shard_map/ppermute | solution.py:253
  251.0 2.1 norm.17
  253.1 2.0 norm.18
  255.1 2.0 norm.19
  261.9 23.9 %all-gather = bf16[16,4,2048]{2,1,0:T(4,128)(2,1)} all-gather(bf16[1,4,2048]{2,1,0:T(4,128)(2,1)S(1)} %maximum_bitcast_fusion), channel_id=1, replica_groups=mesh['bank'=16,'zero'=2] {'bank'}, dimensions={0}, use_global_device_ids=true | all-gather | bytes 278528 | tf_op jit(solution)/shard_map/all_gather | solution.py:315
  285.8 1.7 reshape.36
  287.5 2.1 norm.20
  290.3 3.8 %norm.21 = (bf16[384,1024]{1,0:T(8,128)(2,1)}, bf16[5632,2048]{1,0:T(8,128)(2,1)}) custom-call(f32[5632,1024]{1,0:T(8,128)} %bitcast.23, bf16[5632,1024]{1,0:T(8,128)(2,1)} %bitcast.38, f32[3,1,128]{2,1,0:T(1,128)S(1)} %get-tuple-element.30.own_ref, f32[3,1,128]{2,1,0:T(1,128)S(1)} %collective-permute-done.other_ref, ...), custom_call_target="tpu_custom_call", output_to_operand_aliasing={{1}: (4, {})} | custom-call | flops 1152000 | bytes 1024 | tf_op jit(solution)/shard_map/norm/pallas_call | solution.py:208
  300.0 2.9 place.18._
  303.0 2.9 place.19._
  305.9 2.6 place.20._
  308.5 2.0 place.21._
  310.5 1.7 place.22._
  312.2 1.7 place.23._
  313.9 1.6 place.24._
  315.5 1.6 place.25
  (66 shorter events, 23.4 us)
Async XLA Ops:
  3.7 4.6 %collective-permute-start = (f32[3,1,128]{2,1,0:T(1,128)S(1)}, f32[3,1,128]{2,1,0:T(1,128)S(1)}, u32[]{:S(2)}, u32[]{:S(2)}) collective-permute-start(f32[3,1,128]{2,1,0:T(1,128)S(1)} %get-tuple-element.30.own_ref), channel_id=1, source_target_pairs={{0,1},{1,0},{2,3},{3,2},{4,5},{5,4},{6,7},{7,6},{8,9},{9,8},{10,11... | collective-permute-start | bytes 4616 | tf_op jit(solution)/shard_map/ppermute | solution.py:253
  13.1 4.1 %collective-permute-start.1 = (f32[12,1,128]{2,1,0:T(1,128)S(1)}, f32[12,1,128]{2,1,0:T(1,128)S(1)}, u32[]{:S(2)}, u32[]{:S(2)}) collective-permute-start(f32[12,1,128]{2,1,0:T(1,128)S(1)} %sums.2.own_ref), channel_id=1, source_target_pairs={{0,1},{1,0},{2,3},{3,2},{4,5},{5,4},{6,7},{7,6},{8,9},{9,8},{10,11... | collective-permute-start | bytes 18440 | tf_op jit(solution)/shard_map/ppermute | solution.py:253
  15.2 8.2 %collective-permute-start.15 = (f32[1,1,128]{2,1,0:T(1,128)S(1)}, f32[1,1,128]{2,1,0:T(1,128)S(1)}, u32[]{:S(2)}, u32[]{:S(2)}) collective-permute-start(f32[1,1,128]{2,1,0:T(1,128)S(1)} %get-tuple-element.49.own_ref), channel_id=1, source_target_pairs={{0,1},{1,0},{2,3},{3,2},{4,5},{5,4},{6,7},{7,6},{8,9},{9,8},{10,11... | collective-permute-start | bytes 1544 | tf_op jit(solution)/shard_map/ppermute | solution.py:253
  15.3 82.5 %collective-permute-start.17 = (f32[32,1024]{1,0:T(8,128)S(1)}, f32[32,1024]{1,0:T(8,128)S(1)}, u32[]{:S(2)}, u32[]{:S(2)}) collective-permute-start(f32[32,1024]{1,0:T(8,128)S(1)} %get-tuple-element.28.refs_2_), channel_id=1, source_target_pairs={{0,1},{1,0},{2,3},{3,2},{4,5},{5,4},{6,7},{7,6},{8,9},{9,8},{10,11... | collective-permute-start | bytes 393224 | tf_op jit(solution)/shard_map/ppermute | solution.py:253
  21.7 13.7 %copy-start.6 = (f32[1024,4]{0,1:T(4,128)S(1)}, f32[1024,4]{0,1:T(4,128)}, u32[]{:S(2)}) copy-start(f32[1024,4]{0,1:T(4,128)} %param.6) | copy-start | bytes 49156
  21.7 13.7 %copy-start.7 = (f32[1024]{0:T(1024)S(1)}, f32[1024]{0:T(1024)}, u32[]{:S(2)}) copy-start(f32[1024]{0:T(1024)} %param.7) | copy-start | bytes 12292
  21.7 236.7 %collective-permute-start.12 = (bf16[1024,1024]{1,0:T(8,128)(2,1)}, bf16[1024,1024]{1,0:T(8,128)(2,1)S(1)}, u32[]{:S(2)}, u32[]{:S(2)}) collective-permute-start(bf16[1024,1024]{1,0:T(8,128)(2,1)} %get-tuple-element.31.refs_2_), channel_id=1, source_target_pairs={{0,1},{1,0},{2,3},{3,2},{4,5},{5,4},{6,7},{7,6},{8,9},{9,8},{10,11... | collective-permute-start | bytes 6291464 | tf_op jit(solution)/shard_map/ppermute | solution.py:253
  23.5 75.6 %collective-permute-start.16 = (bf16[96,1024]{1,0:T(8,128)(2,1)S(1)}, bf16[96,1024]{1,0:T(8,128)(2,1)S(1)}, u32[]{:S(2)}, u32[]{:S(2)}) collective-permute-start(bf16[96,1024]{1,0:T(8,128)(2,1)S(1)} %head_norm.5), channel_id=1, source_target_pairs={{0,1},{1,0},{2,3},{3,2},{4,5},{5,4},{6,7},{7,6},{8,9},{9,8},{10,11... | collective-permute-start | bytes 589832 | tf_op jit(solution)/shard_map/ppermute | solution.py:253
  24.0 170.0 %collective-permute-start.14 = (bf16[256,1024]{1,0:T(8,128)(2,1)S(1)}, bf16[256,1024]{1,0:T(8,128)(2,1)S(1)}, u32[]{:S(2)}, u32[]{:S(2)}) collective-permute-start(bf16[256,1024]{1,0:T(8,128)(2,1)S(1)} %head_norm.3.refs_2_), channel_id=1, source_target_pairs={{0,1},{1,0},{2,3},{3,2},{4,5},{5,4},{6,7},{7,6},{8,9},{9,8},{10,11... | collective-permute-start | bytes 1572872 | tf_op jit(solution)/shard_map/ppermute | solution.py:253
  34.9 48.2 %collective-permute-start.2 = (f32[28,1,128]{2,1,0:T(1,128)S(1)}, f32[28,1,128]{2,1,0:T(1,128)S(1)}, u32[]{:S(2)}, u32[]{:S(2)}) collective-permute-start(f32[28,1,128]{2,1,0:T(1,128)S(1)} %sums.3.own_ref), channel_id=1, source_target_pairs={{0,1},{1,0},{2,3},{3,2},{4,5},{5,4},{6,7},{7,6},{8,9},{9,8},{10,11... | collective-permute-start | bytes 43016 | tf_op jit(solution)/shard_map/ppermute | solution.py:253
  83.2 13.8 %collective-permute-start.18 = (bf16[1024,4]{0,1:T(4,128)(2,1)S(1)}, bf16[1024,4]{0,1:T(4,128)(2,1)S(1)}, u32[]{:S(2)}, u32[]{:S(2)}) collective-permute-start(bf16[1024,4]{0,1:T(4,128)(2,1)S(1)} %multiply_convert_fusion), channel_id=1, source_target_pairs={{0,1},{1,0},{2,3},{3,2},{4,5},{5,4},{6,7},{7,6},{8,9},{9,8},{10,11... | collective-permute-start | bytes 24584 | tf_op jit(solution)/shard_map/ppermute | solution.py:253
  97.0 162.9 %collective-permute-start.9 = (bf16[1024,1024]{1,0:T(8,128)(2,1)}, bf16[1024,1024]{1,0:T(8,128)(2,1)}, u32[]{:S(2)}, u32[]{:S(2)}) collective-permute-start(bf16[1024,1024]{1,0:T(8,128)(2,1)} %get-tuple-element.45), channel_id=1, source_target_pairs={{0,1},{1,0},{2,3},{3,2},{4,5},{5,4},{6,7},{7,6},{8,9},{9,8},{10,11... | collective-permute-start | bytes 6291464 | tf_op jit(solution)/shard_map/ppermute | solution.py:253
  97.7 7.2 %copy-start.4 = (f32[32,1024]{1,0:T(8,128)}, f32[32,1024]{1,0:T(8,128)S(1)}, u32[]{:S(2)}) copy-start(f32[32,1024]{1,0:T(8,128)S(1)} %collective-permute-done.17.recv_ref) | copy-start | bytes 393220
  97.7 163.5 %collective-permute-start.10 = (bf16[1024,1024]{1,0:T(8,128)(2,1)}, bf16[1024,1024]{1,0:T(8,128)(2,1)}, u32[]{:S(2)}, u32[]{:S(2)}) collective-permute-start(bf16[1024,1024]{1,0:T(8,128)(2,1)} %get-tuple-element.46), channel_id=1, source_target_pairs={{0,1},{1,0},{2,3},{3,2},{4,5},{5,4},{6,7},{7,6},{8,9},{9,8},{10,11... | collective-permute-start | bytes 6291464 | tf_op jit(solution)/shard_map/ppermute | solution.py:253
  99.2 5.8 %copy-start.2 = (bf16[96,1024]{1,0:T(8,128)(2,1)}, bf16[96,1024]{1,0:T(8,128)(2,1)S(1)}, u32[]{:S(2)}) copy-start(bf16[96,1024]{1,0:T(8,128)(2,1)S(1)} %collective-permute-done.16.recv_ref) | copy-start | bytes 589828
  99.2 94.1 %collective-permute-start.13 = (bf16[128,1024]{1,0:T(8,128)(2,1)S(1)}, bf16[128,1024]{1,0:T(8,128)(2,1)S(1)}, u32[]{:S(2)}, u32[]{:S(2)}) collective-permute-start(bf16[128,1024]{1,0:T(8,128)(2,1)S(1)} %head_norm.4), channel_id=1, source_target_pairs={{0,1},{1,0},{2,3},{3,2},{4,5},{5,4},{6,7},{7,6},{8,9},{9,8},{10,11... | collective-permute-start | bytes 786440 | tf_op jit(solution)/shard_map/ppermute | solution.py:253
  193.2 63.9 %collective-permute-start.8 = (bf16[768,1024]{1,0:T(8,128)(2,1)}, bf16[768,1024]{1,0:T(8,128)(2,1)}, u32[]{:S(2)}, u32[]{:S(2)}) collective-permute-start(bf16[768,1024]{1,0:T(8,128)(2,1)} %get-tuple-element.44), channel_id=1, source_target_pairs={{0,1},{1,0},{2,3},{3,2},{4,5},{5,4},{6,7},{7,6},{8,9},{9,8},{10,11... | collective-permute-start | bytes 4718600 | tf_op jit(solution)/shard_map/ppermute | solution.py:253
  194.0 0.8 copy-start
  194.8 55.5 %collective-permute-start.11 = (bf16[512,1024]{1,0:T(8,128)(2,1)}, bf16[512,1024]{1,0:T(8,128)(2,1)S(1)}, u32[]{:S(2)}, u32[]{:S(2)}) collective-permute-start(bf16[512,1024]{1,0:T(8,128)(2,1)} %get-tuple-element.47), channel_id=1, source_target_pairs={{0,1},{1,0},{2,3},{3,2},{4,5},{5,4},{6,7},{7,6},{8,9},{9,8},{10,11... | collective-permute-start | bytes 3145736 | tf_op jit(solution)/shard_map/ppermute | solution.py:253
  250.3 58.2 %collective-permute-start.7 = (bf16[384,1024]{1,0:T(8,128)(2,1)}, bf16[384,1024]{1,0:T(8,128)(2,1)}, u32[]{:S(2)}, u32[]{:S(2)}) collective-permute-start(bf16[384,1024]{1,0:T(8,128)(2,1)} %get-tuple-element.43), channel_id=1, source_target_pairs={{0,1},{1,0},{2,3},{3,2},{4,5},{5,4},{6,7},{7,6},{8,9},{9,8},{10,11... | collective-permute-start | bytes 2359304 | tf_op jit(solution)/shard_map/ppermute | solution.py:253
  257.1 55.1 %collective-permute-start.5 = (bf16[128,1024]{1,0:T(8,128)(2,1)}, bf16[128,1024]{1,0:T(8,128)(2,1)}, u32[]{:S(2)}, u32[]{:S(2)}) collective-permute-start(bf16[128,1024]{1,0:T(8,128)(2,1)} %get-tuple-element.41), channel_id=1, source_target_pairs={{0,1},{1,0},{2,3},{3,2},{4,5},{5,4},{6,7},{7,6},{8,9},{9,8},{10,11... | collective-permute-start | bytes 786440 | tf_op jit(solution)/shard_map/ppermute | solution.py:253
  258.4 52.1 %collective-permute-start.6 = (bf16[128,1024]{1,0:T(8,128)(2,1)}, bf16[128,1024]{1,0:T(8,128)(2,1)}, u32[]{:S(2)}, u32[]{:S(2)}) collective-permute-start(bf16[128,1024]{1,0:T(8,128)(2,1)} %get-tuple-element.42), channel_id=1, source_target_pairs={{0,1},{1,0},{2,3},{3,2},{4,5},{5,4},{6,7},{7,6},{8,9},{9,8},{10,11... | collective-permute-start | bytes 786440 | tf_op jit(solution)/shard_map/ppermute | solution.py:253
  259.9 54.0 %collective-permute-start.4 = (bf16[64,1024]{1,0:T(8,128)(2,1)}, bf16[64,1024]{1,0:T(8,128)(2,1)}, u32[]{:S(2)}, u32[]{:S(2)}) collective-permute-start(bf16[64,1024]{1,0:T(8,128)(2,1)} %get-tuple-element.53), channel_id=1, source_target_pairs={{0,1},{1,0},{2,3},{3,2},{4,5},{5,4},{6,7},{7,6},{8,9},{9,8},{10,11... | collective-permute-start | bytes 393224 | tf_op jit(solution)/shard_map/ppermute | solution.py:253
  261.2 54.3 %collective-permute-start.3 = (bf16[64,1024]{1,0:T(8,128)(2,1)}, bf16[64,1024]{1,0:T(8,128)(2,1)}, u32[]{:S(2)}, u32[]{:S(2)}) collective-permute-start(bf16[64,1024]{1,0:T(8,128)(2,1)} %get-tuple-element.54), channel_id=1, source_target_pairs={{0,1},{1,0},{2,3},{3,2},{4,5},{5,4},{6,7},{7,6},{8,9},{9,8},{10,11... | collective-permute-start | bytes 393224 | tf_op jit(solution)/shard_map/ppermute | solution.py:253
  290.3 3.8 %copy-start.5 = (f32[32,1024]{1,0:T(8,128)S(1)}, f32[32,1024]{1,0:T(8,128)}, u32[]{:S(2)}) copy-start(f32[32,1024]{1,0:T(8,128)} %copy-done.4) | copy-start | bytes 393220
  294.1 0.9 copy-start.3
  295.0 1.1 copy-start.1

commit v3 on v2

--- a/solution.py
+++ b/solution.py
@@ -13,7 +13,9 @@
 ANY = pl.BlockSpec(memory_space=pl.ANY)
 VMEM = pl.BlockSpec(memory_space=pltpu.VMEM)
 EARLY = 32
-GROUPS = ((1,), (2, 1), (8, 4))
+HEAD, NEXT = 2, 6
+LONG = 8
+LAST = (64, 32, 32)
 LEAST = 24
 
 
@@ -21,8 +23,8 @@
     return pl.CostEstimate(flops=int(us * 1e6), bytes_accessed=1024, transcendentals=0)
 
 
-def params():
-    return pltpu.CompilerParams(vmem_limit_bytes=16 * 1024 * 1024)
+def params(mib):
+    return pltpu.CompilerParams(vmem_limit_bytes=mib * 1024 * 1024)
 
 
 def lane_tiles(ref):
@@ -66,17 +68,17 @@
         sums_ref[b] = jnp.sum(acc.T, axis=0, keepdims=True)
 
 
-def head_norm_kernel(first, merged_ref, own_ref, other_ref, *refs):
-    send_ref = refs[-1]
-    count, row = send_ref.shape[0], first
-    while row < first + count:
-        b, skip = row // LANES, row % LANES
-        rows = min(LANES - skip, first + count - row)
-        inverse = row_scales(own_ref[b], other_ref[b])[skip : skip + rows]
-        for cols in lane_tiles(merged_ref):
-            v = merged_ref[pl.ds(row, rows), cols] * inverse
-            send_ref[pl.ds(row - first, rows), cols] = v.astype(jnp.bfloat16)
-        row += rows
+def head_norm_kernel(cuts, merged_ref, own_ref, other_ref, *send_refs):
+    for (first, count), send_ref in zip(cuts, send_refs, strict=True):
+        row = first
+        while row < first + count:
+            b, skip = row // LANES, row % LANES
+            rows = min(LANES - skip, first + count - row)
+            inverse = row_scales(own_ref[b], other_ref[b])[skip : skip + rows]
+            for cols in lane_tiles(merged_ref):
+                v = merged_ref[pl.ds(row, rows), cols] * inverse
+                send_ref[pl.ds(row - first, rows), cols] = v.astype(jnp.bfloat16)
+            row += rows
 
 
 def sums_kernel(m_ref, s_ref, *refs):
@@ -121,12 +123,24 @@
     copy.wait()
 
 
+def scale_kernel(inner, *refs):
+    out_ref = refs[-1]
+    block = 0
+    for own_ref, other_ref in zip(refs[:-1:2], refs[1:-1:2], strict=True):
+        for b in range(own_ref.shape[0]):
+            expert, at = divmod(block * LANES, inner)
+            out_ref[pl.ds(expert, 1), pl.ds(at, LANES)] = jnp.sqrt(own_ref[b] + other_ref[b])
+            block += 1
+
+
+def router_kernel(gathered_ref, out_ref):
+    devices, columns, _ = gathered_ref.shape
+    for d in range(devices):
+        out_ref[pl.ds(d * columns, columns), :] = gathered_ref[d]
+
+
 def in_hbm(x):
     return pltpu.with_memory_space_constraint(x, pltpu.HBM)
-
-
-def in_vmem(x):
-    return pltpu.with_memory_space_constraint(x, pltpu.VMEM)
 
 
 def whole_of(m):
@@ -142,7 +156,7 @@
     shapes = [sums_shape(blocks), jax.ShapeDtypeStruct((rows, width), jnp.float32)]
     shapes += [jax.ShapeDtypeStruct((early, width), jnp.float32)] if early else []
     return pl.pallas_call(
-        functools.partial(head_kernel, first, early) if not after else after_of(functools.partial(head_kernel, first, early), 2, len(after)),
+        after_of(functools.partial(head_kernel, first, early), 2, len(after)),
         in_specs=[ANY, ANY] + [ANY] * len(after),
         out_specs=[VMEM] * len(shapes),
         out_shape=shapes,
@@ -151,7 +165,7 @@
             pltpu.VMEM((rows, width), s.dtype),
             pltpu.SemaphoreType.DMA((2 * blocks,)),
         ],
-        compiler_params=params(),
+        compiler_params=params(12),
         cost_estimate=cost(1),
         name="head",
     )(m, s, *after)
@@ -164,16 +178,42 @@
     return held
 
 
-def head_norm_of(merged, own, other, first, count):
-    return pl.pallas_call(
-        functools.partial(head_norm_kernel, first),
+def head_norm_of(merged, own, other, cuts):
+    return pl.pallas_call(
+        functools.partial(head_norm_kernel, cuts),
         in_specs=[VMEM] * 3,
-        out_specs=VMEM,
-        out_shape=jax.ShapeDtypeStruct((count, merged.shape[1]), jnp.bfloat16),
-        compiler_params=params(),
+        out_specs=[VMEM] * len(cuts),
+        out_shape=[jax.ShapeDtypeStruct((count, merged.shape[1]), jnp.bfloat16) for _, count in cuts],
+        compiler_params=params(8),
         cost_estimate=cost(1),
         name="head_norm",
     )(merged, own, other)
+
+
+def scale_of(sums, experts, inner):
+    refs = [x for pair in sums for x in pair]
+    return pl.pallas_call(
+        functools.partial(scale_kernel, inner),
+        in_specs=[VMEM] * len(refs),
+        out_specs=VMEM,
+        out_shape=jax.ShapeDtypeStruct((experts, inner), jnp.float32),
+        compiler_params=params(2),
+        cost_estimate=cost(1),
+        name="scale",
+    )(*refs)
+
+
+def router_of(gathered):
+    devices, columns, rows = gathered.shape
+    return pl.pallas_call(
+        router_kernel,
+        in_specs=[VMEM],
+        out_specs=VMEM,
+        out_shape=jax.ShapeDtypeStruct((devices * columns, rows), gathered.dtype),
+        compiler_params=params(4),
+        cost_estimate=cost(1),
+        name="router",
+    )(gathered)
 
 
 def step_rows(*counts):
@@ -193,7 +233,7 @@
         in_specs=[block, block, ANY],
         out_specs=pl.BlockSpec((rows // LANES, 1, LANES), lambda i: (i, 0, 0)),
         out_shape=sums_shape(count // LANES),
-        compiler_params=params(),
+        compiler_params=params(12),
         cost_estimate=cost(count * 0.002),
         name="sums",
     )(m, s, after)
@@ -215,7 +255,7 @@
         ],
         out_shape=[jax.ShapeDtypeStruct((count, width), jnp.bfloat16), whole_of(m)],
         input_output_aliases={4: 1} if held else {},
-        compiler_params=params(),
+        compiler_params=params(14),
         cost_estimate=cost(count * 0.003),
         name="norm",
     )(m, s, own, other, *held)
@@ -229,7 +269,7 @@
         out_shape=jax.ShapeDtypeStruct(out.shape, out.dtype),
         scratch_shapes=[pltpu.SemaphoreType.DMA],
         input_output_aliases={1: 0},
-        compiler_params=params(),
+        compiler_params=params(6),
         cost_estimate=cost(1),
         name="place",
     )(recv, out)
@@ -243,7 +283,7 @@
         out_shape=jax.ShapeDtypeStruct(out.shape, out.dtype),
         scratch_shapes=[pltpu.VMEM(recv.shape, jnp.bfloat16), pltpu.SemaphoreType.DMA],
         input_output_aliases={3: 0},
-        compiler_params=params(),
+        compiler_params=params(2),
         cost_estimate=cost(1),
         name="place_early",
     )(recv, own, other, out)
@@ -253,74 +293,72 @@
     return lax.ppermute(x, "zero", PAIR)
 
 
-def last_cuts(blocks):
+def long_cuts(blocks):
     sizes = []
-    while blocks > 12:
-        sizes.append(8)
-        blocks -= 8
+    while blocks > LONG + 4:
+        sizes.append(LONG)
+        blocks -= LONG
     while blocks > 1:
-        sizes.append(blocks // 2)
-        blocks -= blocks // 2
-    return (*sizes, 1)
-
-
-def plan(blocks):
-    return (*GROUPS, last_cuts(blocks - sum(map(sum, GROUPS))))
+        sizes.append((blocks + 1) // 2)
+        blocks //= 2
+    return sizes + [1] * blocks
 
 
 def pair_steps(master_down, second_down, router_weight, router_gain):
     experts, inner, width = master_down.shape
     n = experts * inner
     m, s = in_hbm(master_down.reshape(n, width)), in_hbm(second_down.reshape(n, width))
-    groups = plan(n // LANES)
-
-    own0, merged0, early = head_of(m, s, 0, 1, EARLY)
-    sums = [(own0, swap(own0))]
+    head, near = HEAD * LANES, (HEAD + NEXT) * LANES
+    recvs = []
+
+    own0, merged0, early = head_of(m, s, 0, HEAD, EARLY)
+    sums0 = own0, swap(own0)
     other_early = swap(early)
-    own1, merged1 = head_of(m, s, LANES, sum(groups[1]), 0, (early,))
-    sums.append((own1, swap(own1)))
-    heads = (merged0, merged1)
-
-    out, recvs, row, i = None, [], 0, 0
-    for g, chunks in enumerate(groups):
-        base = row
-        for c, size in enumerate(chunks):
-            count = size * LANES
-            if g < 2:
-                skip = EARLY if row == 0 else 0
-                send = head_norm_of(heads[g], *sums[g], row - base + skip, count - skip)
-            else:
-                skip = 0
-                send, out = norm_of(m, s, *sums[g], base, row, count, out)
-            if row + count < n:
-                recvs.append((row + skip, swap(send)))
-            else:
-                half = count // 2
-                recvs.append((row, swap(send[:half])))
-                recvs.append((row + half, swap(send[half:])))
-            row += count
-            if g + 1 == len(sums) and g + 1 < len(groups) and c + 1 == max(1, len(chunks) - 1):
-                first, rest = base + sum(chunks) * LANES, sum(groups[g + 1]) * LANES
-                own = sums_of(m, s, first, rest, send)
-                sums.append((own, swap(own)))
-            i += 1
-
-    _, out = norm_of(m, s, *sums[0], 0, 0, LANES, out)
-    _, out = norm_of(m, s, *sums[1], LANES, LANES, sum(groups[1]) * LANES, out)
-
-    part_router = (router_weight * router_gain[:, None]).astype(jnp.bfloat16)
-    me = lax.axis_index("zero")
+    half = EARLY + (head - EARLY) // 32 * 16
+    send_a, send_b = head_norm_of(merged0, *sums0, ((EARLY, half - EARLY), (half, head - half)))
+    recvs.append((EARLY, swap(send_a)))
+    own1, merged1 = head_of(m, s, head, NEXT, 0, (send_a,))
+    sums1 = own1, swap(own1)
+    recvs.append((half, swap(send_b)))
+
+    half = NEXT // 2 * LANES
+    (send_a,) = head_norm_of(merged1, *sums1, ((0, half),))
+    recvs.append((head, swap(send_a)))
+    own2 = sums_of(m, s, near, n - near, send_a)
+    sums2 = own2, swap(own2)
+    (send_b,) = head_norm_of(merged1, *sums1, ((half, NEXT * LANES - half),))
+    recvs.append((head + half, swap(send_b)))
+    part_router = (router_weight.T * router_gain).astype(jnp.bfloat16)
     other_router = swap(part_router)
-    low, high = jnp.where(me == 0, part_router, other_router), jnp.where(me == 0, other_router, part_router)
-    serve_router = lax.all_gather(jnp.concatenate([low, high], 0), "bank", axis=1, tiled=True)
-
-    out = place_early(other_early, *sums[0], out)
-    for row, recv in recvs[:-1]:
+
+    out, row, label = None, near, 4
+    for size in long_cuts(n // LANES - HEAD - NEXT - 1):
+        send, out = norm_of(m, s, *sums2, near, row, size * LANES, out)
+        recvs.append((row, swap(send)))
+        row += size * LANES
+        label += 1
+    cuts, at = [], 0
+    for rows in LAST:
+        cuts.append((at, rows))
+        at += rows
+    _, merged = head_of(m, s, n - LANES, 1, 0, (send,))
+    sends = head_norm_of(merged, *(x[-1:] for x in sums2), tuple(cuts))
+    for (at, _), send in zip(cuts, sends, strict=True):
+        recvs.append((n - LANES + at, swap(send)))
+        label += 1
+
+    _, out = norm_of(m, s, *sums0, 0, 0, head, out)
+    _, out = norm_of(m, s, *sums1, head, head, near - head, out)
+    _, out = norm_of(m, s, *sums2, near, n - LANES, LANES, out)
+    scale_down = scale_of((sums0, sums1, sums2), experts, inner)
+
+    first = lax.axis_index("zero") == 0
+    low, high = jnp.where(first, part_router, other_router), jnp.where(first, other_router, part_router)
+    serve_router = router_of(lax.all_gather(jnp.concatenate([low, high], 1), "bank")).T
+
+    out = place_early(other_early, *sums0, out)
+    for row, recv in recvs:
         out = place(recv, out, row)
-    row, recv = recvs[-1]
-    out = place(in_vmem(recv), out, row)
-    total = jnp.concatenate([own + other for own, other in sums], 0)
-    scale_down = jnp.sqrt(total).reshape(experts, inner)
     return out.reshape(experts, inner, 2 * width), scale_down, serve_router
 
 
@@ -348,7 +386,7 @@
     def step(master_down, *rest):
         experts, inner, width = master_down.shape
         blocks, over = divmod(experts // mesh.shape["bank"] * inner, LANES)
-        if mesh.shape["zero"] != 2 or over or blocks < LEAST or width % (2 * LANES):
+        if mesh.shape["zero"] != 2 or over or blocks < LEAST or inner % LANES or width % LANES:
             return general(master_down, *rest)
         return jax.shard_map(pair_steps, **specs)(master_down, *rest)
 

time: 318 us -> 322 us (1.013)
  local copies, waits for them, and re-layouts: 4.49 us -> 0.52 us
  starting transfers between devices: 22.3 us -> 25.8 us
    pallas_call x5 -> x9, Pallas kernels: 3.47 us -> 8.67 us  [the longest x3 5.85 us: head_of(): pl.pallas_call(after_of(functools.partial(head_kernel, first, early), 2,...]
    ppermute x19, starting transfers between devices: 22.3 us -> 25.8 us  [swap(): return lax.ppermute(x, 'zero', PAIR)]
    pallas_call x2 -> x1, Pallas kernels: 13.9 us -> 11.7 us  [sums_of(): pl.pallas_call(after_of(sums_kernel, 2, 1), grid=(count // rows,), in_spe...]
    pallas_call x11 -> x10, Pallas kernels: 37.6 us -> 36.1 us  [norm_of(): pl.pallas_call(norm_kernel, grid=(count // rows,), in_specs=[block, block...]
    pallas_call x13 -> x14, Pallas kernels: 21.4 us -> 22.8 us  [place(): pl.pallas_call(functools.partial(place_kernel, row), in_specs=[VMEM, ANY]...]
  transfers between devices with their start and end apart: 19 -> 19, of which waited for: 4 -> 7; matrix products, arithmetic and copies ran while one was open for 1% -> 0% of each run, Pallas kernels for 21% -> 23%
where the time goes in v3:
time: 322 us; the launch traced here: 321 us
  waiting for transfers between devices  191 us (59%)
  Pallas kernels  80 us (25%)
  starting transfers between devices  25.8 us (8%)
  blocking collectives  22.3 us (7%)
    ppermute x19, waiting for transfers between devices, swap(): return lax.ppermute(x, 'zero', PAIR)  191 us
    pallas_call x10, Pallas kernels, norm_of(): pl.pallas_call(norm_kernel, grid=(count // rows,), in_specs=[block, block...  36.1 us
    ppermute x19, starting transfers between devices, swap(): return lax.ppermute(x, 'zero', PAIR)  25.8 us
    pallas_call x14, Pallas kernels, place(): pl.pallas_call(functools.partial(place_kernel, row), in_specs=[VMEM, ANY]...  22.8 us
    all_gather x1, blocking collectives, pair_steps(): lax.all_gather(jnp.concatenate([low, high], 1), 'bank')  22.3 us
    pallas_call x1, Pallas kernels, sums_of(): pl.pallas_call(after_of(sums_kernel, 2, 1), grid=(count // rows,), in_spe...  11.7 us
  transfers between devices with their start and end apart: 19, of which 7 were waited for; matrix products, arithmetic and copies ran while one was open for 0% of the time, Pallas kernels for 23%

profile of v3, /device:TPU:0, one launch (start us, length us, event | category | flops | bytes accessed | tf_op | source)
XLA Modules:
  0.0 321.2 jit_solution(1662856119280363910)
XLA Ops:
  2.2 3.1 collective-permute-start
  6.9 2.5 head.4
  9.5 2.1 collective-permute-start.1
  13.4 2.1 collective-permute-start.13
  15.7 11.7 %sums.1.own_ref.refs_4_ = f32[36,1,128]{2,1,0:T(1,128)S(1)} custom-call(f32[5632,1024]{1,0:T(8,128)} %bitcast.13, bf16[5632,1024]{1,0:T(8,128)(2,1)} %bitcast.27, bf16[384,1024]{1,0:T(8,128)(2,1)S(1)} %head_norm.5.refs_2_), custom_call_target="tpu_custom_call" | custom-call | flops 9216000 | bytes 1024 | tf_op jit(solution)/shard_map/sums/pallas_call | solution.py:230
  27.5 2.0 collective-permute-start.17
  29.5 4.7 %collective-permute-done.2.other_ref.refs_5_ = f32[36,1,128]{2,1,0:T(1,128)S(1)} collective-permute-done((f32[36,1,128]{2,1,0:T(1,128)S(1)}, f32[36,1,128]{2,1,0:T(1,128)S(1)}, u32[]{:S(2)}, u32[]{:S(2)}) %collective-permute-start.2) | collective-permute-done | bytes 18464 | tf_op jit(solution)/shard_map/ppermute | solution.py:293
  34.3 4.5 %norm.10 = (bf16[1024,1024]{1,0:T(8,128)(2,1)}, bf16[5632,2048]{1,0:T(8,128)(2,1)}) custom-call(f32[5632,1024]{1,0:T(8,128)} %bitcast.14, bf16[5632,1024]{1,0:T(8,128)(2,1)} %bitcast.28, f32[36,1,128]{2,1,0:T(1,128)S(1)} %sums.1.own_ref.refs_4_, f32[36,1,128]{2,1,0:T(1,128)S(1)} %collective-permute-done.2.other_ref.refs_5_), custom_call_target="tpu_custom_call" | custom-call | flops 3072000 | bytes 1024 | tf_op jit(solution)/shard_map/norm/pallas_call | solution.py:248
  38.7 4.5 %norm.11 = (bf16[1024,1024]{1,0:T(8,128)(2,1)}, bf16[5632,2048]{1,0:T(8,128)(2,1)}) custom-call(f32[5632,1024]{1,0:T(8,128)} %bitcast.15, bf16[5632,1024]{1,0:T(8,128)(2,1)} %bitcast.29, f32[36,1,128]{2,1,0:T(1,128)S(1)} %sums.1.own_ref.refs_4_, f32[36,1,128]{2,1,0:T(1,128)S(1)} %collective-permute-done.2.other_ref.refs_5_, ...), custom_call_target="tpu_custom_call", output_to_operand_aliasing={{1}: (4, {})} | custom-call | flops 3072000 | bytes 1024 | tf_op jit(solution)/shard_map/norm/pallas_call | solution.py:248
  43.2 4.5 %norm.12 = (bf16[1024,1024]{1,0:T(8,128)(2,1)}, bf16[5632,2048]{1,0:T(8,128)(2,1)}) custom-call(f32[5632,1024]{1,0:T(8,128)} %bitcast.16, bf16[5632,1024]{1,0:T(8,128)(2,1)} %bitcast.30, f32[36,1,128]{2,1,0:T(1,128)S(1)} %sums.1.own_ref.refs_4_, f32[36,1,128]{2,1,0:T(1,128)S(1)} %collective-permute-done.2.other_ref.refs_5_, ...), custom_call_target="tpu_custom_call", output_to_operand_aliasing={{1}: (4, {})} | custom-call | flops 3072000 | bytes 1024 | tf_op jit(solution)/shard_map/norm/pallas_call | solution.py:248
  47.7 2.0 collective-permute-start.10
  49.9 43.8 %collective-permute-done.18 = bf16[4,1024]{1,0:T(4,128)(2,1)S(1)} collective-permute-done((bf16[4,1024]{1,0:T(4,128)(2,1)S(1)}, bf16[4,1024]{1,0:T(4,128)(2,1)S(1)}, u32[]{:S(2)}, u32[]{:S(2)}) %collective-permute-start.18) | collective-permute-done | bytes 8224 | tf_op jit(solution)/shard_map/ppermute | solution.py:293
  93.7 2.0 collective-permute-start.11
  97.8 91.7 %collective-permute-done.16.recv_ref = bf16[112,1024]{1,0:T(8,128)(2,1)S(1)} collective-permute-done((bf16[112,1024]{1,0:T(8,128)(2,1)S(1)}, bf16[112,1024]{1,0:T(8,128)(2,1)S(1)}, u32[]{:S(2)}, u32[]{:S(2)}) %collective-permute-start.16) | collective-permute-done | bytes 229408 | tf_op jit(solution)/shard_map/ppermute | solution.py:293
  189.5 2.0 collective-permute-start.14
  191.5 5.0 %norm.13 = (bf16[768,1024]{1,0:T(8,128)(2,1)}, bf16[5632,2048]{1,0:T(8,128)(2,1)}) custom-call(f32[5632,1024]{1,0:T(8,128)} %bitcast.17, bf16[5632,1024]{1,0:T(8,128)(2,1)} %bitcast.31, f32[36,1,128]{2,1,0:T(1,128)S(1)} %sums.1.own_ref.refs_4_, f32[36,1,128]{2,1,0:T(1,128)S(1)} %collective-permute-done.2.other_ref.refs_5_, ...), custom_call_target="tpu_custom_call", output_to_operand_aliasing={{1}: (4, {})} | custom-call | flops 2304000 | bytes 1024 | tf_op jit(solution)/shard_map/norm/pallas_call | solution.py:248
  196.6 3.9 %norm.14 = (bf16[384,1024]{1,0:T(8,128)(2,1)}, bf16[5632,2048]{1,0:T(8,128)(2,1)}) custom-call(f32[5632,1024]{1,0:T(8,128)} %bitcast.18, bf16[5632,1024]{1,0:T(8,128)(2,1)} %bitcast.32, f32[36,1,128]{2,1,0:T(1,128)S(1)} %sums.1.own_ref.refs_4_, f32[36,1,128]{2,1,0:T(1,128)S(1)} %collective-permute-done.2.other_ref.refs_5_, ...), custom_call_target="tpu_custom_call", output_to_operand_aliasing={{1}: (4, {})} | custom-call | flops 1152000 | bytes 1024 | tf_op jit(solution)/shard_map/norm/pallas_call | solution.py:248
  200.5 9.4 %collective-permute-done.14.recv_ref = bf16[384,1024]{1,0:T(8,128)(2,1)S(1)} collective-permute-done((bf16[384,1024]{1,0:T(8,128)(2,1)S(1)}, bf16[384,1024]{1,0:T(8,128)(2,1)S(1)}, u32[]{:S(2)}, u32[]{:S(2)}) %collective-permute-start.14) | collective-permute-done | bytes 786464 | tf_op jit(solution)/shard_map/ppermute | solution.py:293
  209.9 2.0 collective-permute-start.8
  212.6 2.1 norm.15
  214.7 2.1 norm.16
  219.3 38.2 %collective-permute-done.8.recv_ref = bf16[384,1024]{1,0:T(8,128)(2,1)} collective-permute-done((bf16[384,1024]{1,0:T(8,128)(2,1)}, bf16[384,1024]{1,0:T(8,128)(2,1)}, u32[]{:S(2)}, u32[]{:S(2)}) %collective-permute-start.8) | collective-permute-done | bytes 786464 | tf_op jit(solution)/shard_map/ppermute | solution.py:293
  257.5 2.0 collective-permute-start.6
  259.6 2.0 collective-permute-start.5
  263.7 22.3 %all-gather.1.gathered_ref = bf16[16,4,2048]{2,1,0:T(4,128)(2,1)S(1)} all-gather(bf16[1,4,2048]{2,1,0:T(4,128)(2,1)S(1)} %maximum_bitcast_fusion), channel_id=2, replica_groups=mesh['bank'=16,'zero'=2] {'bank'}, dimensions={0}, use_global_device_ids=true | all-gather | bytes 278528 | tf_op jit(solution)/shard_map/all_gather | solution.py:357
  286.8 2.5 norm.17
  289.3 5.0 %norm.18 = (bf16[768,1024]{1,0:T(8,128)(2,1)}, bf16[5632,2048]{1,0:T(8,128)(2,1)}) custom-call(f32[5632,1024]{1,0:T(8,128)} %bitcast.23, bf16[5632,1024]{1,0:T(8,128)(2,1)} %bitcast.37, f32[6,1,128]{2,1,0:T(1,128)S(1)} %get-tuple-element.35.own_ref.refs_2_, ...), custom_call_target="tpu_custom_call", output_to_operand_aliasing={{1}: (4, {})} | custom-call | flops 2304000 | bytes 1024 | tf_op jit(solution)/shard_map/norm/pallas_call | solution.py:248
  294.3 2.1 norm.19
  301.5 2.9 place.18._
  304.4 2.9 place.19._
  308.7 2.6 place.21._
  311.3 2.0 place.22._
  (57 shorter events, 28.1 us)
Async XLA Ops:
  2.2 4.6 %collective-permute-start = (f32[2,1,128]{2,1,0:T(1,128)S(1)}, f32[2,1,128]{2,1,0:T(1,128)S(1)}, u32[]{:S(2)}, u32[]{:S(2)}) collective-permute-start(f32[2,1,128]{2,1,0:T(1,128)S(1)} %get-tuple-element.32.own_ref.refs_0_), channel_id=1, source_target_pairs={{0,1},{1,0},{2,3},{3,2},{4,5},{5,4},{6,7},{7,6},{8,9},{9,8},{10,11... | collective-permute-start | bytes 3080 | tf_op jit(solution)/shard_map/ppermute | solution.py:293
  9.5 3.7 %collective-permute-start.1 = (f32[6,1,128]{2,1,0:T(1,128)S(1)}, f32[6,1,128]{2,1,0:T(1,128)S(1)}, u32[]{:S(2)}, u32[]{:S(2)}) collective-permute-start(f32[6,1,128]{2,1,0:T(1,128)S(1)} %get-tuple-element.35.own_ref.refs_2_), channel_id=1, source_target_pairs={{0,1},{1,0},{2,3},{3,2},{4,5},{5,4},{6,7},{7,6},{8,9},{9,8},{10,11... | collective-permute-start | bytes 9224 | tf_op jit(solution)/shard_map/ppermute | solution.py:293
  13.4 183.1 %collective-permute-start.13 = (bf16[384,1024]{1,0:T(8,128)(2,1)S(1)}, bf16[384,1024]{1,0:T(8,128)(2,1)S(1)}, u32[]{:S(2)}, u32[]{:S(2)}) collective-permute-start(bf16[384,1024]{1,0:T(8,128)(2,1)S(1)} %head_norm.7), channel_id=1, source_target_pairs={{0,1},{1,0},{2,3},{3,2},{4,5},{5,4},{6,7},{7,6},{8,9},{9,8},{10,11... | collective-permute-start | bytes 2359304 | tf_op jit(solution)/shard_map/ppermute | solution.py:293
  27.4 6.9 %collective-permute-start.2 = (f32[36,1,128]{2,1,0:T(1,128)S(1)}, f32[36,1,128]{2,1,0:T(1,128)S(1)}, u32[]{:S(2)}, u32[]{:S(2)}) collective-permute-start(f32[36,1,128]{2,1,0:T(1,128)S(1)} %sums.1.own_ref.refs_4_), channel_id=1, source_target_pairs={{0,1},{1,0},{2,3},{3,2},{4,5},{5,4},{6,7},{7,6},{8,9},{9,8},{10,11... | collective-permute-start | bytes 55304 | tf_op jit(solution)/shard_map/ppermute | solution.py:293
  27.5 68.3 %collective-permute-start.17 = (f32[32,1024]{1,0:T(8,128)S(1)}, f32[32,1024]{1,0:T(8,128)S(1)}, u32[]{:S(2)}, u32[]{:S(2)}) collective-permute-start(f32[32,1024]{1,0:T(8,128)S(1)} %get-tuple-element.54), channel_id=1, source_target_pairs={{0,1},{1,0},{2,3},{3,2},{4,5},{5,4},{6,7},{7,6},{8,9},{9,8},{10,11... | collective-permute-start | bytes 393224 | tf_op jit(solution)/shard_map/ppermute | solution.py:293
  29.5 66.3 %collective-permute-start.15 = (bf16[112,1024]{1,0:T(8,128)(2,1)S(1)}, bf16[112,1024]{1,0:T(8,128)(2,1)S(1)}, u32[]{:S(2)}, u32[]{:S(2)}) collective-permute-start(bf16[112,1024]{1,0:T(8,128)(2,1)S(1)} %get-tuple-element.53), channel_id=1, source_target_pairs={{0,1},{1,0},{2,3},{3,2},{4,5},{5,4},{6,7},{7,6},{8,9},{9,8},{10,11... | collective-permute-start | bytes 688136 | tf_op jit(solution)/shard_map/ppermute | solution.py:293
  43.2 6.5 %copy-start.2 = (f32[1024,4]{0,1:T(4,128)S(1)}, f32[1024,4]{0,1:T(4,128)}, u32[]{:S(2)}) copy-start(f32[1024,4]{0,1:T(4,128)} %param.6) | copy-start | bytes 49156
  43.2 6.5 %copy-start.3 = (f32[1024]{0:T(1024)S(1)}, f32[1024]{0:T(1024)}, u32[]{:S(2)}) copy-start(f32[1024]{0:T(1024)} %param.7) | copy-start | bytes 12292
  47.7 211.8 %collective-permute-start.10 = (bf16[1024,1024]{1,0:T(8,128)(2,1)}, bf16[1024,1024]{1,0:T(8,128)(2,1)S(1)}, u32[]{:S(2)}, u32[]{:S(2)}) collective-permute-start(bf16[1024,1024]{1,0:T(8,128)(2,1)} %get-tuple-element.50), channel_id=1, source_target_pairs={{0,1},{1,0},{2,3},{3,2},{4,5},{5,4},{6,7},{7,6},{8,9},{9,8},{10,11... | collective-permute-start | bytes 6291464 | tf_op jit(solution)/shard_map/ppermute | solution.py:293
  49.8 43.9 %collective-permute-start.18 = (bf16[4,1024]{1,0:T(4,128)(2,1)S(1)}, bf16[4,1024]{1,0:T(4,128)(2,1)S(1)}, u32[]{:S(2)}, u32[]{:S(2)}) collective-permute-start(bf16[4,1024]{1,0:T(4,128)(2,1)S(1)} %fusion), channel_id=1, source_target_pairs={{0,1},{1,0},{2,3},{3,2},{4,5},{5,4},{6,7},{7,6},{8,9},{9,8},{10,11... | collective-permute-start | bytes 24584 | tf_op jit(solution)/shard_map/ppermute | solution.py:293
  93.7 97.8 %copy-start.4 = (bf16[4,1024]{1,0:T(4,128)(2,1)}, bf16[4,1024]{1,0:T(4,128)(2,1)S(1)}, u32[]{:S(2)}) copy-start(bf16[4,1024]{1,0:T(4,128)(2,1)S(1)} %collective-permute-done.18) | copy-start | bytes 24580
  93.7 167.9 %collective-permute-start.11 = (bf16[1024,1024]{1,0:T(8,128)(2,1)}, bf16[1024,1024]{1,0:T(8,128)(2,1)}, u32[]{:S(2)}, u32[]{:S(2)}) collective-permute-start(bf16[1024,1024]{1,0:T(8,128)(2,1)} %get-tuple-element.51), channel_id=1, source_target_pairs={{0,1},{1,0},{2,3},{3,2},{4,5},{5,4},{6,7},{7,6},{8,9},{9,8},{10,11... | collective-permute-start | bytes 6291464 | tf_op jit(solution)/shard_map/ppermute | solution.py:293
  95.7 166.0 %collective-permute-start.12 = (bf16[1024,1024]{1,0:T(8,128)(2,1)}, bf16[1024,1024]{1,0:T(8,128)(2,1)}, u32[]{:S(2)}, u32[]{:S(2)}) collective-permute-start(bf16[1024,1024]{1,0:T(8,128)(2,1)} %get-tuple-element.52), channel_id=1, source_target_pairs={{0,1},{1,0},{2,3},{3,2},{4,5},{5,4},{6,7},{7,6},{8,9},{9,8},{10,11... | collective-permute-start | bytes 6291464 | tf_op jit(solution)/shard_map/ppermute | solution.py:293
  95.8 93.7 %collective-permute-start.16 = (bf16[112,1024]{1,0:T(8,128)(2,1)S(1)}, bf16[112,1024]{1,0:T(8,128)(2,1)S(1)}, u32[]{:S(2)}, u32[]{:S(2)}) collective-permute-start(bf16[112,1024]{1,0:T(8,128)(2,1)S(1)} %get-tuple-element.33.refs_2_), channel_id=1, source_target_pairs={{0,1},{1,0},{2,3},{3,2},{4,5},{5,4},{6,7},{7,6},{8,9},{9,8},{10,11... | collective-permute-start | bytes 688136 | tf_op jit(solution)/shard_map/ppermute | solution.py:293
  189.5 20.4 %collective-permute-start.14 = (bf16[384,1024]{1,0:T(8,128)(2,1)S(1)}, bf16[384,1024]{1,0:T(8,128)(2,1)S(1)}, u32[]{:S(2)}, u32[]{:S(2)}) collective-permute-start(bf16[384,1024]{1,0:T(8,128)(2,1)S(1)} %head_norm.5.refs_2_), channel_id=1, source_target_pairs={{0,1},{1,0},{2,3},{3,2},{4,5},{5,4},{6,7},{7,6},{8,9},{9,8},{10,11... | collective-permute-start | bytes 2359304 | tf_op jit(solution)/shard_map/ppermute | solution.py:293
  196.5 4.0 %copy-start = (bf16[384,1024]{1,0:T(8,128)(2,1)}, bf16[384,1024]{1,0:T(8,128)(2,1)S(1)}, u32[]{:S(2)}) copy-start(bf16[384,1024]{1,0:T(8,128)(2,1)S(1)} %collective-permute-done.13.recv_ref) | copy-start | bytes 2359300
  196.5 63.1 %collective-permute-start.9 = (bf16[768,1024]{1,0:T(8,128)(2,1)}, bf16[768,1024]{1,0:T(8,128)(2,1)}, u32[]{:S(2)}, u32[]{:S(2)}) collective-permute-start(bf16[768,1024]{1,0:T(8,128)(2,1)} %get-tuple-element.49), channel_id=1, source_target_pairs={{0,1},{1,0},{2,3},{3,2},{4,5},{5,4},{6,7},{7,6},{8,9},{9,8},{10,11... | collective-permute-start | bytes 4718600 | tf_op jit(solution)/shard_map/ppermute | solution.py:293
  209.9 47.6 %collective-permute-start.8 = (bf16[384,1024]{1,0:T(8,128)(2,1)}, bf16[384,1024]{1,0:T(8,128)(2,1)}, u32[]{:S(2)}, u32[]{:S(2)}) collective-permute-start(bf16[384,1024]{1,0:T(8,128)(2,1)} %get-tuple-element.48), channel_id=1, source_target_pairs={{0,1},{1,0},{2,3},{3,2},{4,5},{5,4},{6,7},{7,6},{8,9},{9,8},{10,11... | collective-permute-start | bytes 2359304 | tf_op jit(solution)/shard_map/ppermute | solution.py:293
  257.5 57.5 %collective-permute-start.6 = (bf16[128,1024]{1,0:T(8,128)(2,1)}, bf16[128,1024]{1,0:T(8,128)(2,1)}, u32[]{:S(2)}, u32[]{:S(2)}) collective-permute-start(bf16[128,1024]{1,0:T(8,128)(2,1)} %get-tuple-element.42.refs_2_), channel_id=1, source_target_pairs={{0,1},{1,0},{2,3},{3,2},{4,5},{5,4},{6,7},{7,6},{8,9},{9,8},{10,11... | collective-permute-start | bytes 786440 | tf_op jit(solution)/shard_map/ppermute | solution.py:293
  259.5 53.8 %collective-permute-start.7 = (bf16[128,1024]{1,0:T(8,128)(2,1)}, bf16[128,1024]{1,0:T(8,128)(2,1)}, u32[]{:S(2)}, u32[]{:S(2)}) collective-permute-start(bf16[128,1024]{1,0:T(8,128)(2,1)} %get-tuple-element.47), channel_id=1, source_target_pairs={{0,1},{1,0},{2,3},{3,2},{4,5},{5,4},{6,7},{7,6},{8,9},{9,8},{10,11... | collective-permute-start | bytes 786440 | tf_op jit(solution)/shard_map/ppermute | solution.py:293
  259.6 57.1 %collective-permute-start.5 = (bf16[64,1024]{1,0:T(8,128)(2,1)}, bf16[64,1024]{1,0:T(8,128)(2,1)}, u32[]{:S(2)}, u32[]{:S(2)}) collective-permute-start(bf16[64,1024]{1,0:T(8,128)(2,1)} %get-tuple-element.46), channel_id=1, source_target_pairs={{0,1},{1,0},{2,3},{3,2},{4,5},{5,4},{6,7},{7,6},{8,9},{9,8},{10,11... | collective-permute-start | bytes 393224 | tf_op jit(solution)/shard_map/ppermute | solution.py:293
  261.6 58.2 %collective-permute-start.3 = (bf16[32,1024]{1,0:T(8,128)(2,1)}, bf16[32,1024]{1,0:T(8,128)(2,1)}, u32[]{:S(2)}, u32[]{:S(2)}) collective-permute-start(bf16[32,1024]{1,0:T(8,128)(2,1)} %get-tuple-element.44), channel_id=1, source_target_pairs={{0,1},{1,0},{2,3},{3,2},{4,5},{5,4},{6,7},{7,6},{8,9},{9,8},{10,11... | collective-permute-start | bytes 196616 | tf_op jit(solution)/shard_map/ppermute | solution.py:293
  261.7 56.5 %collective-permute-start.4 = (bf16[32,1024]{1,0:T(8,128)(2,1)}, bf16[32,1024]{1,0:T(8,128)(2,1)}, u32[]{:S(2)}, u32[]{:S(2)}) collective-permute-start(bf16[32,1024]{1,0:T(8,128)(2,1)} %get-tuple-element.45), channel_id=1, source_target_pairs={{0,1},{1,0},{2,3},{3,2},{4,5},{5,4},{6,7},{7,6},{8,9},{9,8},{10,11... | collective-permute-start | bytes 196616 | tf_op jit(solution)/shard_map/ppermute | solution.py:293
  299.2 1.4 copy-start.1

commit v4 on v3

--- a/solution.py
+++ b/solution.py
@@ -12,9 +12,10 @@
 PAIR = ((0, 1), (1, 0))
 ANY = pl.BlockSpec(memory_space=pl.ANY)
 VMEM = pl.BlockSpec(memory_space=pltpu.VMEM)
-EARLY = 32
+EARLY = 48
 HEAD, NEXT = 2, 6
 LONG = 8
+AHEAD = 12
 LAST = (64, 32, 32)
 LEAST = 24
 
@@ -133,6 +134,13 @@
             block += 1
 
 
+def router_rows_kernel(own_ref, other_ref, out_ref):
+    width = own_ref.shape[1]
+    me = lax.axis_index("zero")
+    for ref, at in ((own_ref, me), (other_ref, 1 - me)):
+        out_ref[:, pl.ds(pl.multiple_of(at * width, LANES), width)] = ref[...]
+
+
 def router_kernel(gathered_ref, out_ref):
     devices, columns, _ = gathered_ref.shape
     for d in range(devices):
@@ -201,6 +209,18 @@
         cost_estimate=cost(1),
         name="scale",
     )(*refs)
+
+
+def router_rows_of(own, other):
+    return pl.pallas_call(
+        router_rows_kernel,
+        in_specs=[VMEM] * 2,
+        out_specs=VMEM,
+        out_shape=jax.ShapeDtypeStruct((own.shape[0], 2 * own.shape[1]), own.dtype),
+        compiler_params=params(2),
+        cost_estimate=cost(1),
+        name="router_rows",
+    )(own, other)
 
 
 def router_of(gathered):
@@ -331,8 +351,23 @@
     part_router = (router_weight.T * router_gain).astype(jnp.bfloat16)
     other_router = swap(part_router)
 
+    rows = router_rows_of(part_router, other_router)
+    serve_router = router_of(lax.all_gather(rows, "bank")).T
+
+    def ready(out, ahead):
+        if recvs[0][0] == EARLY:
+            _, out = norm_of(m, s, *sums0, 0, 0, head, out)
+            _, out = norm_of(m, s, *sums1, head, head, near - head, out)
+            out = place_early(other_early, *sums0, out)
+        while recvs and sum(recv.shape[0] for _, recv in recvs[1:]) >= ahead:
+            at, recv = recvs.pop(0)
+            out = place(recv, out, at)
+        return out
+
     out, row, label = None, near, 4
     for size in long_cuts(n // LANES - HEAD - NEXT - 1):
+        if label > 5:
+            out = ready(out, AHEAD * LANES)
         send, out = norm_of(m, s, *sums2, near, row, size * LANES, out)
         recvs.append((row, swap(send)))
         row += size * LANES
@@ -346,19 +381,9 @@
     for (at, _), send in zip(cuts, sends, strict=True):
         recvs.append((n - LANES + at, swap(send)))
         label += 1
-
-    _, out = norm_of(m, s, *sums0, 0, 0, head, out)
-    _, out = norm_of(m, s, *sums1, head, head, near - head, out)
     _, out = norm_of(m, s, *sums2, near, n - LANES, LANES, out)
     scale_down = scale_of((sums0, sums1, sums2), experts, inner)
-
-    first = lax.axis_index("zero") == 0
-    low, high = jnp.where(first, part_router, other_router), jnp.where(first, other_router, part_router)
-    serve_router = router_of(lax.all_gather(jnp.concatenate([low, high], 1), "bank")).T
-
-    out = place_early(other_early, *sums0, out)
-    for row, recv in recvs:
-        out = place(recv, out, row)
+    out = ready(out, 0)
     return out.reshape(experts, inner, 2 * width), scale_down, serve_router
 
 

time: 322 us -> 325 us (level)
  waiting for transfers between devices: 191 us -> 209 us
  Pallas kernels: 80 us -> 66.9 us
    ppermute x19, waiting for transfers between devices: 191 us -> 209 us  [swap(): return lax.ppermute(x, 'zero', PAIR)]
    pallas_call x14, Pallas kernels: 22.8 us -> 12.7 us  [place(): pl.pallas_call(functools.partial(place_kernel, row), in_specs=[VMEM, ANY]...]
  transfers between devices with their start and end apart: 19 -> 19, of which waited for: 7 -> 6; matrix products, arithmetic and copies ran while one was open for 0% -> 0% of each run, Pallas kernels for 23% -> 14%
where the time goes in v4:
time: 325 us
  waiting for transfers between devices  209 us (64%)
  Pallas kernels  66.9 us (21%)
  starting transfers between devices  25.6 us (8%)
  blocking collectives  22.3 us (7%)
    ppermute x19, waiting for transfers between devices, swap(): return lax.ppermute(x, 'zero', PAIR)  209 us
    pallas_call x10, Pallas kernels, norm_of(): pl.pallas_call(norm_kernel, grid=(count // rows,), in_specs=[block, block...  33.8 us
    ppermute x19, starting transfers between devices, swap(): return lax.ppermute(x, 'zero', PAIR)  25.6 us
    all_gather x1, blocking collectives, pair_steps(): serve_router = router_of(lax.all_gather(rows, 'bank')).T  22.3 us
    pallas_call x14, Pallas kernels, place(): pl.pallas_call(functools.partial(place_kernel, row), in_specs=[VMEM, ANY]...  12.7 us
    pallas_call x1, Pallas kernels, sums_of(): pl.pallas_call(after_of(sums_kernel, 2, 1), grid=(count // rows,), in_spe...  11.7 us
  transfers between devices with their start and end apart: 19, of which 6 were waited for; matrix products, arithmetic and copies ran while one was open for 0% of the time, Pallas kernels for 14%

profile of v4, /device:TPU:0, one launch (start us, length us, event | category | flops | bytes accessed | tf_op | source)
XLA Modules:
  0.0 324.7 jit_solution(4339422985961883311)
XLA Ops:
  2.2 3.1 collective-permute-start
  5.2 1.6 collective-permute-done.other_ref.refs_1_
  6.9 2.5 head.4
  9.5 2.1 collective-permute-start.1
  11.6 1.6 collective-permute-done.1.other_ref.refs_3_
  13.4 11.7 %sums.1.own_ref.refs_4_ = f32[36,1,128]{2,1,0:T(1,128)S(1)} custom-call(f32[5632,1024]{1,0:T(8,128)} %bitcast.11, bf16[5632,1024]{1,0:T(8,128)(2,1)} %bitcast.25, bf16[384,1024]{1,0:T(8,128)(2,1)S(1)} %head_norm.5.refs_2_), custom_call_target="tpu_custom_call" | custom-call | flops 9216000 | bytes 1024 | tf_op jit(solution)/shard_map/sums/pallas_call | solution.py:250
  25.1 2.1 collective-permute-start.2
  27.2 1.7 collective-permute-done.2.other_ref.refs_5_
  28.9 4.1 %norm.10 = (bf16[1024,1024]{1,0:T(8,128)(2,1)S(1)}, bf16[5632,2048]{1,0:T(8,128)(2,1)}) custom-call(f32[5632,1024]{1,0:T(8,128)} %bitcast.12, bf16[5632,1024]{1,0:T(8,128)(2,1)} %bitcast.26, f32[36,1,128]{2,1,0:T(1,128)S(1)} %sums.1.own_ref.refs_4_, f32[36,1,128]{2,1,0:T(1,128)S(1)} %collective-permute-done.2.other_ref.refs_5_), custom_call_target="tpu_custom_call" | custom-call | flops 3072000 | bytes 1024 | tf_op jit(solution)/shard_map/norm/pallas_call | solution.py:268
  33.0 2.0 collective-permute-start.4
  35.3 2.1 collective-permute-start.5
  37.4 4.1 %norm.11 = (bf16[1024,1024]{1,0:T(8,128)(2,1)S(1)}, bf16[5632,2048]{1,0:T(8,128)(2,1)}) custom-call(f32[5632,1024]{1,0:T(8,128)} %bitcast.13, bf16[5632,1024]{1,0:T(8,128)(2,1)} %bitcast.27, f32[36,1,128]{2,1,0:T(1,128)S(1)} %sums.1.own_ref.refs_4_, f32[36,1,128]{2,1,0:T(1,128)S(1)} %collective-permute-done.2.other_ref.refs_5_, ...), custom_call_target="tpu_custom_call", output_to_operand_aliasing={{1}: (4, {})} | custom-call | flops 3072000 | bytes 1024 | tf_op jit(solution)/shard_map/norm/pallas_call | solution.py:268
  41.5 2.0 collective-permute-start.9
  43.5 118.2 %collective-permute-done.9.recv_ref = f32[48,1024]{1,0:T(8,128)S(1)} collective-permute-done((f32[48,1024]{1,0:T(8,128)S(1)}, f32[48,1024]{1,0:T(8,128)S(1)}, u32[]{:S(2)}, u32[]{:S(2)}) %collective-permute-start.9) | collective-permute-done | bytes 196640 | tf_op jit(solution)/shard_map/ppermute | solution.py:313
  161.7 2.0 collective-permute-start.8
  163.7 5.5 %collective-permute-done.8.recv_ref = bf16[96,1024]{1,0:T(8,128)(2,1)S(1)} collective-permute-done((bf16[96,1024]{1,0:T(8,128)(2,1)S(1)}, bf16[96,1024]{1,0:T(8,128)(2,1)S(1)}, u32[]{:S(2)}, u32[]{:S(2)}) %collective-permute-start.8) | collective-permute-done | bytes 196640 | tf_op jit(solution)/shard_map/ppermute | solution.py:313
  169.2 1.7 collective-permute-start.7
  171.0 2.5 norm.12
  173.5 5.0 %norm.13 = (bf16[768,1024]{1,0:T(8,128)(2,1)}, bf16[5632,2048]{1,0:T(8,128)(2,1)}) custom-call(f32[5632,1024]{1,0:T(8,128)} %bitcast.15, bf16[5632,1024]{1,0:T(8,128)(2,1)} %bitcast.29, f32[6,1,128]{2,1,0:T(1,128)S(1)} %get-tuple-element.35.own_ref.refs_2_, ...), custom_call_target="tpu_custom_call", output_to_operand_aliasing={{1}: (4, {})} | custom-call | flops 2304000 | bytes 1024 | tf_op jit(solution)/shard_map/norm/pallas_call | solution.py:268
  182.5 4.2 %norm.14 = (bf16[1024,1024]{1,0:T(8,128)(2,1)S(1)}, bf16[5632,2048]{1,0:T(8,128)(2,1)}) custom-call(f32[5632,1024]{1,0:T(8,128)} %bitcast.16, bf16[5632,1024]{1,0:T(8,128)(2,1)} %bitcast.30, f32[36,1,128]{2,1,0:T(1,128)S(1)} %sums.1.own_ref.refs_4_, f32[36,1,128]{2,1,0:T(1,128)S(1)} %collective-permute-done.2.other_ref.refs_5_, ...), custom_call_target="tpu_custom_call", output_to_operand_aliasing={{1}: (4, {})} | custom-call | flops 3072000 | bytes 1024 | tf_op jit(solution)/shard_map/norm/pallas_call | solution.py:268
  188.3 4.4 %norm.15 = (bf16[768,1024]{1,0:T(8,128)(2,1)S(1)}, bf16[5632,2048]{1,0:T(8,128)(2,1)}) custom-call(f32[5632,1024]{1,0:T(8,128)} %bitcast.17, bf16[5632,1024]{1,0:T(8,128)(2,1)} %bitcast.31, f32[36,1,128]{2,1,0:T(1,128)S(1)} %sums.1.own_ref.refs_4_, f32[36,1,128]{2,1,0:T(1,128)S(1)} %collective-permute-done.2.other_ref.refs_5_, ...), custom_call_target="tpu_custom_call", output_to_operand_aliasing={{1}: (4, {})} | custom-call | flops 2304000 | bytes 1024 | tf_op jit(solution)/shard_map/norm/pallas_call | solution.py:268
  192.8 1.7 collective-permute-start.16
  195.9 3.5 %norm.16 = (bf16[384,1024]{1,0:T(8,128)(2,1)S(1)}, bf16[5632,2048]{1,0:T(8,128)(2,1)}) custom-call(f32[5632,1024]{1,0:T(8,128)} %bitcast.18, bf16[5632,1024]{1,0:T(8,128)(2,1)} %bitcast.32, f32[36,1,128]{2,1,0:T(1,128)S(1)} %sums.1.own_ref.refs_4_, f32[36,1,128]{2,1,0:T(1,128)S(1)} %collective-permute-done.2.other_ref.refs_5_, ...), custom_call_target="tpu_custom_call", output_to_operand_aliasing={{1}: (4, {})} | custom-call | flops 1152000 | bytes 1024 | tf_op jit(solution)/shard_map/norm/pallas_call | solution.py:268
  199.6 1.8 collective-permute-start.18
  201.4 2.0 norm.17
  203.7 2.0 norm.18
  205.7 80.3 %collective-permute-done.18.other_ref = bf16[4,1024]{1,0:T(4,128)(2,1)S(1)} collective-permute-done((bf16[4,1024]{1,0:T(4,128)(2,1)S(1)}, bf16[4,1024]{1,0:T(4,128)(2,1)S(1)}, u32[]{:S(2)}, u32[]{:S(2)}) %collective-permute-start.18) | collective-permute-done | bytes 8224 | tf_op jit(solution)/shard_map/ppermute | solution.py:313
  286.2 1.8 head.5
  288.2 1.8 collective-permute-start.12
  290.3 1.7 collective-permute-start.11
  292.0 22.3 %all-gather.1.gathered_ref = bf16[16,4,2048]{2,1,0:T(4,128)(2,1)S(1)} all-gather(bf16[1,4,2048]{2,1,0:T(4,128)(2,1)S(1)} %bitcast.7), channel_id=2, replica_groups=mesh['bank'=16,'zero'=2] {'bank'}, dimensions={0}, use_global_device_ids=true | all-gather | bytes 278528 | tf_op jit(solution)/shard_map/all_gather | solution.py:355
  315.7 2.1 norm.19
  (54 shorter events, 18.6 us)
Async XLA Ops:
  2.2 4.6 %collective-permute-start = (f32[2,1,128]{2,1,0:T(1,128)S(1)}, f32[2,1,128]{2,1,0:T(1,128)S(1)}, u32[]{:S(2)}, u32[]{:S(2)}) collective-permute-start(f32[2,1,128]{2,1,0:T(1,128)S(1)} %get-tuple-element.32.own_ref.refs_0_), channel_id=1, source_target_pairs={{0,1},{1,0},{2,3},{3,2},{4,5},{5,4},{6,7},{7,6},{8,9},{9,8},{10,11... | collective-permute-start | bytes 3080 | tf_op jit(solution)/shard_map/ppermute | solution.py:313
  6.8 171.7 %copy-start = (f32[2,1,128]{2,1,0:T(1,128)}, f32[2,1,128]{2,1,0:T(1,128)S(1)}, u32[]{:S(2)}) copy-start(f32[2,1,128]{2,1,0:T(1,128)S(1)} %collective-permute-done.other_ref.refs_1_) | copy-start | bytes 3076
  9.5 3.7 %collective-permute-start.1 = (f32[6,1,128]{2,1,0:T(1,128)S(1)}, f32[6,1,128]{2,1,0:T(1,128)S(1)}, u32[]{:S(2)}, u32[]{:S(2)}) collective-permute-start(f32[6,1,128]{2,1,0:T(1,128)S(1)} %get-tuple-element.35.own_ref.refs_2_), channel_id=1, source_target_pairs={{0,1},{1,0},{2,3},{3,2},{4,5},{5,4},{6,7},{7,6},{8,9},{9,8},{10,11... | collective-permute-start | bytes 9224 | tf_op jit(solution)/shard_map/ppermute | solution.py:313
  25.1 3.8 %collective-permute-start.2 = (f32[36,1,128]{2,1,0:T(1,128)S(1)}, f32[36,1,128]{2,1,0:T(1,128)S(1)}, u32[]{:S(2)}, u32[]{:S(2)}) collective-permute-start(f32[36,1,128]{2,1,0:T(1,128)S(1)} %sums.1.own_ref.refs_4_), channel_id=1, source_target_pairs={{0,1},{1,0},{2,3},{3,2},{4,5},{5,4},{6,7},{7,6},{8,9},{9,8},{10,11... | collective-permute-start | bytes 55304 | tf_op jit(solution)/shard_map/ppermute | solution.py:313
  33.0 153.9 %collective-permute-start.4 = (bf16[1024,1024]{1,0:T(8,128)(2,1)S(1)}, bf16[1024,1024]{1,0:T(8,128)(2,1)S(1)}, u32[]{:S(2)}, u32[]{:S(2)}) collective-permute-start(bf16[1024,1024]{1,0:T(8,128)(2,1)S(1)} %get-tuple-element.38), channel_id=1, source_target_pairs={{0,1},{1,0},{2,3},{3,2},{4,5},{5,4},{6,7},{7,6},{8,9},{9,8},{10,11... | collective-permute-start | bytes 6291464 | tf_op jit(solution)/shard_map/ppermute | solution.py:313
  35.1 145.6 %collective-permute-start.6 = (bf16[384,1024]{1,0:T(8,128)(2,1)S(1)}, bf16[384,1024]{1,0:T(8,128)(2,1)S(1)}, u32[]{:S(2)}, u32[]{:S(2)}) collective-permute-start(bf16[384,1024]{1,0:T(8,128)(2,1)S(1)} %head_norm.5.refs_2_), channel_id=1, source_target_pairs={{0,1},{1,0},{2,3},{3,2},{4,5},{5,4},{6,7},{7,6},{8,9},{9,8},{10,11... | collective-permute-start | bytes 2359304 | tf_op jit(solution)/shard_map/ppermute | solution.py:313
  35.3 146.3 %collective-permute-start.5 = (bf16[384,1024]{1,0:T(8,128)(2,1)S(1)}, bf16[384,1024]{1,0:T(8,128)(2,1)S(1)}, u32[]{:S(2)}, u32[]{:S(2)}) collective-permute-start(bf16[384,1024]{1,0:T(8,128)(2,1)S(1)} %head_norm.6), channel_id=1, source_target_pairs={{0,1},{1,0},{2,3},{3,2},{4,5},{5,4},{6,7},{7,6},{8,9},{9,8},{10,11... | collective-permute-start | bytes 2359304 | tf_op jit(solution)/shard_map/ppermute | solution.py:313
  41.5 153.0 %collective-permute-start.3 = (bf16[1024,1024]{1,0:T(8,128)(2,1)S(1)}, bf16[1024,1024]{1,0:T(8,128)(2,1)S(1)}, u32[]{:S(2)}, u32[]{:S(2)}) collective-permute-start(bf16[1024,1024]{1,0:T(8,128)(2,1)S(1)} %get-tuple-element.37), channel_id=1, source_target_pairs={{0,1},{1,0},{2,3},{3,2},{4,5},{5,4},{6,7},{7,6},{8,9},{9,8},{10,11... | collective-permute-start | bytes 6291464 | tf_op jit(solution)/shard_map/ppermute | solution.py:313
  41.5 120.2 %collective-permute-start.9 = (f32[48,1024]{1,0:T(8,128)S(1)}, f32[48,1024]{1,0:T(8,128)S(1)}, u32[]{:S(2)}, u32[]{:S(2)}) collective-permute-start(f32[48,1024]{1,0:T(8,128)S(1)} %get-tuple-element.40), channel_id=1, source_target_pairs={{0,1},{1,0},{2,3},{3,2},{4,5},{5,4},{6,7},{7,6},{8,9},{9,8},{10,11... | collective-permute-start | bytes 589832 | tf_op jit(solution)/shard_map/ppermute | solution.py:313
  161.7 7.6 %collective-permute-start.8 = (bf16[96,1024]{1,0:T(8,128)(2,1)S(1)}, bf16[96,1024]{1,0:T(8,128)(2,1)S(1)}, u32[]{:S(2)}, u32[]{:S(2)}) collective-permute-start(bf16[96,1024]{1,0:T(8,128)(2,1)S(1)} %get-tuple-element.33.refs_2_), channel_id=1, source_target_pairs={{0,1},{1,0},{2,3},{3,2},{4,5},{5,4},{6,7},{7,6},{8,9},{9,8},{10,11... | collective-permute-start | bytes 589832 | tf_op jit(solution)/shard_map/ppermute | solution.py:313
  169.2 10.7 %collective-permute-start.7 = (bf16[112,1024]{1,0:T(8,128)(2,1)S(1)}, bf16[112,1024]{1,0:T(8,128)(2,1)S(1)}, u32[]{:S(2)}, u32[]{:S(2)}) collective-permute-start(bf16[112,1024]{1,0:T(8,128)(2,1)S(1)} %get-tuple-element.39), channel_id=1, source_target_pairs={{0,1},{1,0},{2,3},{3,2},{4,5},{5,4},{6,7},{7,6},{8,9},{9,8},{10,11... | collective-permute-start | bytes 688136 | tf_op jit(solution)/shard_map/ppermute | solution.py:313
  186.7 101.5 %collective-permute-start.17 = (bf16[1024,1024]{1,0:T(8,128)(2,1)S(1)}, bf16[1024,1024]{1,0:T(8,128)(2,1)S(1)}, u32[]{:S(2)}, u32[]{:S(2)}) collective-permute-start(bf16[1024,1024]{1,0:T(8,128)(2,1)S(1)} %get-tuple-element.56), channel_id=1, source_target_pairs={{0,1},{1,0},{2,3},{3,2},{4,5},{5,4},{6,7},{7,6},{8,9},{9,8},{10,11... | collective-permute-start | bytes 6291464 | tf_op jit(solution)/shard_map/ppermute | solution.py:313
  192.8 97.5 %collective-permute-start.16 = (bf16[768,1024]{1,0:T(8,128)(2,1)S(1)}, bf16[768,1024]{1,0:T(8,128)(2,1)S(1)}, u32[]{:S(2)}, u32[]{:S(2)}) collective-permute-start(bf16[768,1024]{1,0:T(8,128)(2,1)S(1)} %get-tuple-element.55), channel_id=1, source_target_pairs={{0,1},{1,0},{2,3},{3,2},{4,5},{5,4},{6,7},{7,6},{8,9},{9,8},{10,11... | collective-permute-start | bytes 4718600 | tf_op jit(solution)/shard_map/ppermute | solution.py:313
  195.8 3.8 %copy-start.2 = (f32[1024,4]{0,1:T(4,128)S(1)}, f32[1024,4]{0,1:T(4,128)}, u32[]{:S(2)}) copy-start(f32[1024,4]{0,1:T(4,128)} %param.6) | copy-start | bytes 49156
  195.9 3.8 %copy-start.3 = (f32[1024]{0:T(1024)S(1)}, f32[1024]{0:T(1024)}, u32[]{:S(2)}) copy-start(f32[1024]{0:T(1024)} %param.7) | copy-start | bytes 12292
  199.3 90.6 %collective-permute-start.15 = (bf16[384,1024]{1,0:T(8,128)(2,1)S(1)}, bf16[384,1024]{1,0:T(8,128)(2,1)S(1)}, u32[]{:S(2)}, u32[]{:S(2)}) collective-permute-start(bf16[384,1024]{1,0:T(8,128)(2,1)S(1)} %get-tuple-element.54), channel_id=1, source_target_pairs={{0,1},{1,0},{2,3},{3,2},{4,5},{5,4},{6,7},{7,6},{8,9},{9,8},{10,11... | collective-permute-start | bytes 2359304 | tf_op jit(solution)/shard_map/ppermute | solution.py:313
  199.6 86.3 %collective-permute-start.18 = (bf16[4,1024]{1,0:T(4,128)(2,1)S(1)}, bf16[4,1024]{1,0:T(4,128)(2,1)S(1)}, u32[]{:S(2)}, u32[]{:S(2)}) collective-permute-start(bf16[4,1024]{1,0:T(4,128)(2,1)S(1)} %fusion.own_ref), channel_id=1, source_target_pairs={{0,1},{1,0},{2,3},{3,2},{4,5},{5,4},{6,7},{7,6},{8,9},{9,8},{10,11... | collective-permute-start | bytes 24584 | tf_op jit(solution)/shard_map/ppermute | solution.py:313
  203.4 117.8 %collective-permute-start.14 = (bf16[128,1024]{1,0:T(8,128)(2,1)S(1)}, bf16[128,1024]{1,0:T(8,128)(2,1)S(1)}, u32[]{:S(2)}, u32[]{:S(2)}) collective-permute-start(bf16[128,1024]{1,0:T(8,128)(2,1)S(1)} %get-tuple-element.53), channel_id=1, source_target_pairs={{0,1},{1,0},{2,3},{3,2},{4,5},{5,4},{6,7},{7,6},{8,9},{9,8},{10,11... | collective-permute-start | bytes 786440 | tf_op jit(solution)/shard_map/ppermute | solution.py:313
  205.7 109.4 %copy-start.1 = (f32[2,1,128]{2,1,0:T(1,128)S(1)}, f32[2,1,128]{2,1,0:T(1,128)}, u32[]{:S(2)}) copy-start(f32[2,1,128]{2,1,0:T(1,128)} %copy-done) | copy-start | bytes 3076
  285.9 36.0 %collective-permute-start.13 = (bf16[128,1024]{1,0:T(8,128)(2,1)S(1)}, bf16[128,1024]{1,0:T(8,128)(2,1)S(1)}, u32[]{:S(2)}, u32[]{:S(2)}) collective-permute-start(bf16[128,1024]{1,0:T(8,128)(2,1)S(1)} %get-tuple-element.48.refs_2_), channel_id=1, source_target_pairs={{0,1},{1,0},{2,3},{3,2},{4,5},{5,4},{6,7},{7,6},{8,9},{9,8},{10,11... | collective-permute-start | bytes 786440 | tf_op jit(solution)/shard_map/ppermute | solution.py:313
  288.2 34.5 %collective-permute-start.12 = (bf16[64,1024]{1,0:T(8,128)(2,1)S(1)}, bf16[64,1024]{1,0:T(8,128)(2,1)S(1)}, u32[]{:S(2)}, u32[]{:S(2)}) collective-permute-start(bf16[64,1024]{1,0:T(8,128)(2,1)S(1)} %get-tuple-element.52), channel_id=1, source_target_pairs={{0,1},{1,0},{2,3},{3,2},{4,5},{5,4},{6,7},{7,6},{8,9},{9,8},{10,11... | collective-permute-start | bytes 393224 | tf_op jit(solution)/shard_map/ppermute | solution.py:313
  290.0 34.1 %collective-permute-start.10 = (bf16[32,1024]{1,0:T(8,128)(2,1)S(1)}, bf16[32,1024]{1,0:T(8,128)(2,1)S(1)}, u32[]{:S(2)}, u32[]{:S(2)}) collective-permute-start(bf16[32,1024]{1,0:T(8,128)(2,1)S(1)} %get-tuple-element.50), channel_id=1, source_target_pairs={{0,1},{1,0},{2,3},{3,2},{4,5},{5,4},{6,7},{7,6},{8,9},{9,8},{10,11... | collective-permute-start | bytes 196616 | tf_op jit(solution)/shard_map/ppermute | solution.py:313
  290.3 33.1 %collective-permute-start.11 = (bf16[32,1024]{1,0:T(8,128)(2,1)S(1)}, bf16[32,1024]{1,0:T(8,128)(2,1)S(1)}, u32[]{:S(2)}, u32[]{:S(2)}) collective-permute-start(bf16[32,1024]{1,0:T(8,128)(2,1)S(1)} %get-tuple-element.51), channel_id=1, source_target_pairs={{0,1},{1,0},{2,3},{3,2},{4,5},{5,4},{6,7},{7,6},{8,9},{9,8},{10,11... | collective-permute-start | bytes 196616 | tf_op jit(solution)/shard_map/ppermute | solution.py:313

commit v5 on v4

--- a/solution.py
+++ b/solution.py
@@ -12,12 +12,12 @@
 PAIR = ((0, 1), (1, 0))
 ANY = pl.BlockSpec(memory_space=pl.ANY)
 VMEM = pl.BlockSpec(memory_space=pltpu.VMEM)
-EARLY = 48
-HEAD, NEXT = 2, 6
+EARLY = 80
+HEAD, NEXT = 3, 5
 LONG = 8
 AHEAD = 12
 LAST = (64, 32, 32)
-LEAST = 24
+LEAST = 40
 
 
 def cost(us):
@@ -64,7 +64,7 @@
             v = merged_tile(m_ref, s_ref, block_rows(b), cols)
             merged_ref[block_rows(b), cols] = v
             if early and b == 0:
-                refs[2][:, cols] = v[:early]
+                refs[2][:, cols] = v[:early].astype(jnp.bfloat16)
             acc = acc + v * v
         sums_ref[b] = jnp.sum(acc.T, axis=0, keepdims=True)
 
@@ -118,7 +118,7 @@
     rows = recv_ref.shape[0]
     inverse = row_scales(own_ref[0], other_ref[0])[:rows]
     for cols in lane_tiles(recv_ref):
-        held_ref[:, cols] = (recv_ref[:, cols] * inverse).astype(jnp.bfloat16)
+        held_ref[:, cols] = (recv_ref[:, cols].astype(jnp.float32) * inverse).astype(jnp.bfloat16)
     copy = pltpu.make_async_copy(held_ref, received_half(out_ref, 0, recv_ref.shape), sem)
     copy.start()
     copy.wait()
@@ -162,7 +162,7 @@
 def head_of(m, s, first, blocks, early, after=()):
     rows, width = blocks * LANES, m.shape[1]
     shapes = [sums_shape(blocks), jax.ShapeDtypeStruct((rows, width), jnp.float32)]
-    shapes += [jax.ShapeDtypeStruct((early, width), jnp.float32)] if early else []
+    shapes += [jax.ShapeDtypeStruct((early, width), jnp.bfloat16)] if early else []
     return pl.pallas_call(
         after_of(functools.partial(head_kernel, first, early), 2, len(after)),
         in_specs=[ANY, ANY] + [ANY] * len(after),
@@ -341,7 +341,7 @@
     sums1 = own1, swap(own1)
     recvs.append((half, swap(send_b)))
 
-    half = NEXT // 2 * LANES
+    half = (NEXT + 1) // 2 * LANES
     (send_a,) = head_norm_of(merged1, *sums1, ((0, half),))
     recvs.append((head, swap(send_a)))
     own2 = sums_of(m, s, near, n - near, send_a)

time: 325 us -> 313 us (0.963)
  waiting for transfers between devices: 209 us -> 193 us
    ppermute x19, waiting for transfers between devices: 209 us -> 193 us  [swap(): return lax.ppermute(x, 'zero', PAIR)]
  transfers between devices with their start and end apart: 19 -> 19, of which waited for: 6 -> 7; matrix products, arithmetic and copies ran while one was open for 0% -> 0% of each run, Pallas kernels for 14% -> 15%
where the time goes in v5:
time: 313 us; the launch traced here: 312 us
  waiting for transfers between devices  193 us (62%)
  Pallas kernels  68.4 us (22%)
  starting transfers between devices  27.3 us (9%)
  blocking collectives  22.5 us (7%)
    ppermute x19, waiting for transfers between devices, swap(): return lax.ppermute(x, 'zero', PAIR)  193 us
    pallas_call x10, Pallas kernels, norm_of(): pl.pallas_call(norm_kernel, grid=(count // rows,), in_specs=[block, block...  35.3 us
    ppermute x19, starting transfers between devices, swap(): return lax.ppermute(x, 'zero', PAIR)  27.3 us
    all_gather x1, blocking collectives, pair_steps(): serve_router = router_of(lax.all_gather(rows, 'bank')).T  22.5 us
    pallas_call x14, Pallas kernels, place(): pl.pallas_call(functools.partial(place_kernel, row), in_specs=[VMEM, ANY]...  12.6 us
    pallas_call x1, Pallas kernels, sums_of(): pl.pallas_call(after_of(sums_kernel, 2, 1), grid=(count // rows,), in_spe...  11.7 us
  transfers between devices with their start and end apart: 19, of which 7 were waited for; matrix products, arithmetic and copies ran while one was open for 0% of the time, Pallas kernels for 15%

profile of v5, /device:TPU:0, one launch (start us, length us, event | category | flops | bytes accessed | tf_op | source)
XLA Modules:
  0.0 312.0 jit_solution(18081531764484657102)
XLA Ops:
  0.6 1.8 head.3
  2.4 3.1 collective-permute-start
  7.2 2.3 head.4
  9.5 2.1 collective-permute-start.1
  13.4 11.7 %sums.1.own_ref.refs_4_ = f32[36,1,128]{2,1,0:T(1,128)S(1)} custom-call(f32[5632,1024]{1,0:T(8,128)} %bitcast.11, bf16[5632,1024]{1,0:T(8,128)(2,1)} %bitcast.25, bf16[384,1024]{1,0:T(8,128)(2,1)S(1)} %head_norm.5.refs_2_), custom_call_target="tpu_custom_call" | custom-call | flops 9216000 | bytes 1024 | tf_op jit(solution)/shard_map/sums/pallas_call | solution.py:250
  25.1 2.1 collective-permute-start.2
  27.2 1.7 collective-permute-done.2.other_ref.refs_5_
  28.9 4.1 %norm.10 = (bf16[1024,1024]{1,0:T(8,128)(2,1)S(1)}, bf16[5632,2048]{1,0:T(8,128)(2,1)}) custom-call(f32[5632,1024]{1,0:T(8,128)} %bitcast.12, bf16[5632,1024]{1,0:T(8,128)(2,1)} %bitcast.26, f32[36,1,128]{2,1,0:T(1,128)S(1)} %sums.1.own_ref.refs_4_, f32[36,1,128]{2,1,0:T(1,128)S(1)} %collective-permute-done.2.other_ref.refs_5_), custom_call_target="tpu_custom_call" | custom-call | flops 3072000 | bytes 1024 | tf_op jit(solution)/shard_map/norm/pallas_call | solution.py:268
  33.1 2.0 collective-permute-start.4
  35.1 4.1 %norm.11 = (bf16[1024,1024]{1,0:T(8,128)(2,1)S(1)}, bf16[5632,2048]{1,0:T(8,128)(2,1)}) custom-call(f32[5632,1024]{1,0:T(8,128)} %bitcast.13, bf16[5632,1024]{1,0:T(8,128)(2,1)} %bitcast.27, f32[36,1,128]{2,1,0:T(1,128)S(1)} %sums.1.own_ref.refs_4_, f32[36,1,128]{2,1,0:T(1,128)S(1)} %collective-permute-done.2.other_ref.refs_5_, ...), custom_call_target="tpu_custom_call", output_to_operand_aliasing={{1}: (4, {})} | custom-call | flops 3072000 | bytes 1024 | tf_op jit(solution)/shard_map/norm/pallas_call | solution.py:268
  39.2 2.0 collective-permute-start.3
  41.3 2.0 collective-permute-start.8
  43.4 103.4 %collective-permute-done.9.recv_ref = bf16[80,1024]{1,0:T(8,128)(2,1)S(1)} collective-permute-done((bf16[80,1024]{1,0:T(8,128)(2,1)S(1)}, bf16[80,1024]{1,0:T(8,128)(2,1)S(1)}, u32[]{:S(2)}, u32[]{:S(2)}) %collective-permute-start.9) | collective-permute-done | bytes 163872 | tf_op jit(solution)/shard_map/ppermute | solution.py:313
  146.9 2.0 collective-permute-start.5
  148.9 4.3 %collective-permute-done.8.recv_ref = bf16[144,1024]{1,0:T(8,128)(2,1)S(1)} collective-permute-done((bf16[144,1024]{1,0:T(8,128)(2,1)S(1)}, bf16[144,1024]{1,0:T(8,128)(2,1)S(1)}, u32[]{:S(2)}, u32[]{:S(2)}) %collective-permute-start.8) | collective-permute-done | bytes 294944 | tf_op jit(solution)/shard_map/ppermute | solution.py:313
  153.2 2.0 collective-permute-start.7
  155.2 3.7 %norm.12 = (bf16[384,1024]{1,0:T(8,128)(2,1)}, bf16[5632,2048]{1,0:T(8,128)(2,1)}) custom-call(f32[5632,1024]{1,0:T(8,128)} %bitcast.14, bf16[5632,1024]{1,0:T(8,128)(2,1)} %bitcast.28, f32[3,1,128]{2,1,0:T(1,128)S(1)} %get-tuple-element.32.own_ref.refs_0_, f32[3,1,128]{2,1,0:T(1,128)S(1)} %collective-permute-done.other_ref.refs_1_, ...), custom_call_target="tpu_custom_call", output_to_operand_aliasing={{1}: (4, {})} | custom-call | flops 1152000 | bytes 1024 | tf_op jit(solution)/shard_map/norm/pallas_call | solution.py:268
  158.9 5.3 %norm.13 = (bf16[640,1024]{1,0:T(8,128)(2,1)}, bf16[5632,2048]{1,0:T(8,128)(2,1)}) custom-call(f32[5632,1024]{1,0:T(8,128)} %bitcast.15, bf16[5632,1024]{1,0:T(8,128)(2,1)} %bitcast.29, f32[5,1,128]{2,1,0:T(1,128)S(1)} %get-tuple-element.35.own_ref.refs_2_, ...), custom_call_target="tpu_custom_call", output_to_operand_aliasing={{1}: (4, {})} | custom-call | flops 1920000 | bytes 1024 | tf_op jit(solution)/shard_map/norm/pallas_call | solution.py:268
  169.6 4.2 %norm.14 = (bf16[1024,1024]{1,0:T(8,128)(2,1)S(1)}, bf16[5632,2048]{1,0:T(8,128)(2,1)}) custom-call(f32[5632,1024]{1,0:T(8,128)} %bitcast.16, bf16[5632,1024]{1,0:T(8,128)(2,1)} %bitcast.30, f32[36,1,128]{2,1,0:T(1,128)S(1)} %sums.1.own_ref.refs_4_, f32[36,1,128]{2,1,0:T(1,128)S(1)} %collective-permute-done.2.other_ref.refs_5_, ...), custom_call_target="tpu_custom_call", output_to_operand_aliasing={{1}: (4, {})} | custom-call | flops 3072000 | bytes 1024 | tf_op jit(solution)/shard_map/norm/pallas_call | solution.py:268
  173.8 1.7 collective-permute-start.17
  176.9 4.4 %norm.15 = (bf16[768,1024]{1,0:T(8,128)(2,1)S(1)}, bf16[5632,2048]{1,0:T(8,128)(2,1)}) custom-call(f32[5632,1024]{1,0:T(8,128)} %bitcast.17, bf16[5632,1024]{1,0:T(8,128)(2,1)} %bitcast.31, f32[36,1,128]{2,1,0:T(1,128)S(1)} %sums.1.own_ref.refs_4_, f32[36,1,128]{2,1,0:T(1,128)S(1)} %collective-permute-done.2.other_ref.refs_5_, ...), custom_call_target="tpu_custom_call", output_to_operand_aliasing={{1}: (4, {})} | custom-call | flops 2304000 | bytes 1024 | tf_op jit(solution)/shard_map/norm/pallas_call | solution.py:268
  183.0 3.5 %norm.16 = (bf16[384,1024]{1,0:T(8,128)(2,1)S(1)}, bf16[5632,2048]{1,0:T(8,128)(2,1)}) custom-call(f32[5632,1024]{1,0:T(8,128)} %bitcast.18, bf16[5632,1024]{1,0:T(8,128)(2,1)} %bitcast.32, f32[36,1,128]{2,1,0:T(1,128)S(1)} %sums.1.own_ref.refs_4_, f32[36,1,128]{2,1,0:T(1,128)S(1)} %collective-permute-done.2.other_ref.refs_5_, ...), custom_call_target="tpu_custom_call", output_to_operand_aliasing={{1}: (4, {})} | custom-call | flops 1152000 | bytes 1024 | tf_op jit(solution)/shard_map/norm/pallas_call | solution.py:268
  186.4 1.7 collective-permute-start.15
  188.5 2.0 norm.17
  190.5 1.7 collective-permute-start.14
  192.3 2.0 norm.18
  194.2 78.8 %collective-permute-done.18.other_ref = bf16[4,1024]{1,0:T(4,128)(2,1)S(1)} collective-permute-done((bf16[4,1024]{1,0:T(4,128)(2,1)S(1)}, bf16[4,1024]{1,0:T(4,128)(2,1)S(1)}, u32[]{:S(2)}, u32[]{:S(2)}) %collective-permute-start.18) | collective-permute-done | bytes 8224 | tf_op jit(solution)/shard_map/ppermute | solution.py:313
  273.0 1.7 collective-permute-start.13
  274.8 1.8 head.5
  277.1 1.7 collective-permute-start.10
  279.1 22.5 %all-gather.1.gathered_ref = bf16[16,4,2048]{2,1,0:T(4,128)(2,1)S(1)} all-gather(bf16[1,4,2048]{2,1,0:T(4,128)(2,1)S(1)} %bitcast.7), channel_id=2, replica_groups=mesh['bank'=16,'zero'=2] {'bank'}, dimensions={0}, use_global_device_ids=true | all-gather | bytes 278528 | tf_op jit(solution)/shard_map/all_gather | solution.py:355
  303.1 2.1 norm.19
  (54 shorter events, 21.5 us)
Async XLA Ops:
  2.4 4.6 %collective-permute-start = (f32[3,1,128]{2,1,0:T(1,128)S(1)}, f32[3,1,128]{2,1,0:T(1,128)S(1)}, u32[]{:S(2)}, u32[]{:S(2)}) collective-permute-start(f32[3,1,128]{2,1,0:T(1,128)S(1)} %get-tuple-element.32.own_ref.refs_0_), channel_id=1, source_target_pairs={{0,1},{1,0},{2,3},{3,2},{4,5},{5,4},{6,7},{7,6},{8,9},{9,8},{10,11... | collective-permute-start | bytes 4616 | tf_op jit(solution)/shard_map/ppermute | solution.py:313
  7.0 157.2 %copy-start = (f32[3,1,128]{2,1,0:T(1,128)}, f32[3,1,128]{2,1,0:T(1,128)S(1)}, u32[]{:S(2)}) copy-start(f32[3,1,128]{2,1,0:T(1,128)S(1)} %collective-permute-done.other_ref.refs_1_) | copy-start | bytes 4612
  9.5 3.7 %collective-permute-start.1 = (f32[5,1,128]{2,1,0:T(1,128)S(1)}, f32[5,1,128]{2,1,0:T(1,128)S(1)}, u32[]{:S(2)}, u32[]{:S(2)}) collective-permute-start(f32[5,1,128]{2,1,0:T(1,128)S(1)} %get-tuple-element.35.own_ref.refs_2_), channel_id=1, source_target_pairs={{0,1},{1,0},{2,3},{3,2},{4,5},{5,4},{6,7},{7,6},{8,9},{9,8},{10,11... | collective-permute-start | bytes 7688 | tf_op jit(solution)/shard_map/ppermute | solution.py:313
  25.1 3.8 %collective-permute-start.2 = (f32[36,1,128]{2,1,0:T(1,128)S(1)}, f32[36,1,128]{2,1,0:T(1,128)S(1)}, u32[]{:S(2)}, u32[]{:S(2)}) collective-permute-start(f32[36,1,128]{2,1,0:T(1,128)S(1)} %sums.1.own_ref.refs_4_), channel_id=1, source_target_pairs={{0,1},{1,0},{2,3},{3,2},{4,5},{5,4},{6,7},{7,6},{8,9},{9,8},{10,11... | collective-permute-start | bytes 55304 | tf_op jit(solution)/shard_map/ppermute | solution.py:313
  33.1 142.5 %collective-permute-start.4 = (bf16[1024,1024]{1,0:T(8,128)(2,1)S(1)}, bf16[1024,1024]{1,0:T(8,128)(2,1)S(1)}, u32[]{:S(2)}, u32[]{:S(2)}) collective-permute-start(bf16[1024,1024]{1,0:T(8,128)(2,1)S(1)} %get-tuple-element.38), channel_id=1, source_target_pairs={{0,1},{1,0},{2,3},{3,2},{4,5},{5,4},{6,7},{7,6},{8,9},{9,8},{10,11... | collective-permute-start | bytes 6291464 | tf_op jit(solution)/shard_map/ppermute | solution.py:313
  35.1 132.8 %collective-permute-start.6 = (bf16[384,1024]{1,0:T(8,128)(2,1)S(1)}, bf16[384,1024]{1,0:T(8,128)(2,1)S(1)}, u32[]{:S(2)}, u32[]{:S(2)}) collective-permute-start(bf16[384,1024]{1,0:T(8,128)(2,1)S(1)} %head_norm.5.refs_2_), channel_id=1, source_target_pairs={{0,1},{1,0},{2,3},{3,2},{4,5},{5,4},{6,7},{7,6},{8,9},{9,8},{10,11... | collective-permute-start | bytes 2359304 | tf_op jit(solution)/shard_map/ppermute | solution.py:313
  39.2 142.4 %collective-permute-start.3 = (bf16[1024,1024]{1,0:T(8,128)(2,1)S(1)}, bf16[1024,1024]{1,0:T(8,128)(2,1)S(1)}, u32[]{:S(2)}, u32[]{:S(2)}) collective-permute-start(bf16[1024,1024]{1,0:T(8,128)(2,1)S(1)} %get-tuple-element.37), channel_id=1, source_target_pairs={{0,1},{1,0},{2,3},{3,2},{4,5},{5,4},{6,7},{7,6},{8,9},{9,8},{10,11... | collective-permute-start | bytes 6291464 | tf_op jit(solution)/shard_map/ppermute | solution.py:313
  41.2 105.6 %collective-permute-start.9 = (bf16[80,1024]{1,0:T(8,128)(2,1)S(1)}, bf16[80,1024]{1,0:T(8,128)(2,1)S(1)}, u32[]{:S(2)}, u32[]{:S(2)}) collective-permute-start(bf16[80,1024]{1,0:T(8,128)(2,1)S(1)} %get-tuple-element.40), channel_id=1, source_target_pairs={{0,1},{1,0},{2,3},{3,2},{4,5},{5,4},{6,7},{7,6},{8,9},{9,8},{10,11... | collective-permute-start | bytes 491528 | tf_op jit(solution)/shard_map/ppermute | solution.py:313
  41.3 111.9 %collective-permute-start.8 = (bf16[144,1024]{1,0:T(8,128)(2,1)S(1)}, bf16[144,1024]{1,0:T(8,128)(2,1)S(1)}, u32[]{:S(2)}, u32[]{:S(2)}) collective-permute-start(bf16[144,1024]{1,0:T(8,128)(2,1)S(1)} %get-tuple-element.33.refs_2_), channel_id=1, source_target_pairs={{0,1},{1,0},{2,3},{3,2},{4,5},{5,4},{6,7},{7,6},{8,9},{9,8},{10,11... | collective-permute-start | bytes 884744 | tf_op jit(solution)/shard_map/ppermute | solution.py:313
  146.9 21.9 %collective-permute-start.5 = (bf16[256,1024]{1,0:T(8,128)(2,1)S(1)}, bf16[256,1024]{1,0:T(8,128)(2,1)S(1)}, u32[]{:S(2)}, u32[]{:S(2)}) collective-permute-start(bf16[256,1024]{1,0:T(8,128)(2,1)S(1)} %head_norm.6), channel_id=1, source_target_pairs={{0,1},{1,0},{2,3},{3,2},{4,5},{5,4},{6,7},{7,6},{8,9},{9,8},{10,11... | collective-permute-start | bytes 1572872 | tf_op jit(solution)/shard_map/ppermute | solution.py:313
  153.2 14.0 %collective-permute-start.7 = (bf16[160,1024]{1,0:T(8,128)(2,1)S(1)}, bf16[160,1024]{1,0:T(8,128)(2,1)S(1)}, u32[]{:S(2)}, u32[]{:S(2)}) collective-permute-start(bf16[160,1024]{1,0:T(8,128)(2,1)S(1)} %get-tuple-element.39), channel_id=1, source_target_pairs={{0,1},{1,0},{2,3},{3,2},{4,5},{5,4},{6,7},{7,6},{8,9},{9,8},{10,11... | collective-permute-start | bytes 983048 | tf_op jit(solution)/shard_map/ppermute | solution.py:313
  173.8 102.9 %collective-permute-start.17 = (bf16[1024,1024]{1,0:T(8,128)(2,1)S(1)}, bf16[1024,1024]{1,0:T(8,128)(2,1)S(1)}, u32[]{:S(2)}, u32[]{:S(2)}) collective-permute-start(bf16[1024,1024]{1,0:T(8,128)(2,1)S(1)} %get-tuple-element.56), channel_id=1, source_target_pairs={{0,1},{1,0},{2,3},{3,2},{4,5},{5,4},{6,7},{7,6},{8,9},{9,8},{10,11... | collective-permute-start | bytes 6291464 | tf_op jit(solution)/shard_map/ppermute | solution.py:313
  181.3 97.5 %collective-permute-start.16 = (bf16[768,1024]{1,0:T(8,128)(2,1)S(1)}, bf16[768,1024]{1,0:T(8,128)(2,1)S(1)}, u32[]{:S(2)}, u32[]{:S(2)}) collective-permute-start(bf16[768,1024]{1,0:T(8,128)(2,1)S(1)} %get-tuple-element.55), channel_id=1, source_target_pairs={{0,1},{1,0},{2,3},{3,2},{4,5},{5,4},{6,7},{7,6},{8,9},{9,8},{10,11... | collective-permute-start | bytes 4718600 | tf_op jit(solution)/shard_map/ppermute | solution.py:313
  182.9 5.2 %copy-start.2 = (f32[1024,4]{0,1:T(4,128)S(1)}, f32[1024,4]{0,1:T(4,128)}, u32[]{:S(2)}) copy-start(f32[1024,4]{0,1:T(4,128)} %param.6) | copy-start | bytes 49156
  183.0 5.2 %copy-start.3 = (f32[1024]{0:T(1024)S(1)}, f32[1024]{0:T(1024)}, u32[]{:S(2)}) copy-start(f32[1024]{0:T(1024)} %param.7) | copy-start | bytes 12292
  186.4 90.6 %collective-permute-start.15 = (bf16[384,1024]{1,0:T(8,128)(2,1)S(1)}, bf16[384,1024]{1,0:T(8,128)(2,1)S(1)}, u32[]{:S(2)}, u32[]{:S(2)}) collective-permute-start(bf16[384,1024]{1,0:T(8,128)(2,1)S(1)} %get-tuple-element.54), channel_id=1, source_target_pairs={{0,1},{1,0},{2,3},{3,2},{4,5},{5,4},{6,7},{7,6},{8,9},{9,8},{10,11... | collective-permute-start | bytes 2359304 | tf_op jit(solution)/shard_map/ppermute | solution.py:313
  188.2 84.8 %collective-permute-start.18 = (bf16[4,1024]{1,0:T(4,128)(2,1)S(1)}, bf16[4,1024]{1,0:T(4,128)(2,1)S(1)}, u32[]{:S(2)}, u32[]{:S(2)}) collective-permute-start(bf16[4,1024]{1,0:T(4,128)(2,1)S(1)} %fusion.own_ref), channel_id=1, source_target_pairs={{0,1},{1,0},{2,3},{3,2},{4,5},{5,4},{6,7},{7,6},{8,9},{9,8},{10,11... | collective-permute-start | bytes 24584 | tf_op jit(solution)/shard_map/ppermute | solution.py:313
  190.5 118.0 %collective-permute-start.14 = (bf16[128,1024]{1,0:T(8,128)(2,1)S(1)}, bf16[128,1024]{1,0:T(8,128)(2,1)S(1)}, u32[]{:S(2)}, u32[]{:S(2)}) collective-permute-start(bf16[128,1024]{1,0:T(8,128)(2,1)S(1)} %get-tuple-element.53), channel_id=1, source_target_pairs={{0,1},{1,0},{2,3},{3,2},{4,5},{5,4},{6,7},{7,6},{8,9},{9,8},{10,11... | collective-permute-start | bytes 786440 | tf_op jit(solution)/shard_map/ppermute | solution.py:313
  194.2 108.2 %copy-start.1 = (f32[3,1,128]{2,1,0:T(1,128)S(1)}, f32[3,1,128]{2,1,0:T(1,128)}, u32[]{:S(2)}) copy-start(f32[3,1,128]{2,1,0:T(1,128)} %copy-done) | copy-start | bytes 4612
  273.0 36.3 %collective-permute-start.13 = (bf16[128,1024]{1,0:T(8,128)(2,1)S(1)}, bf16[128,1024]{1,0:T(8,128)(2,1)S(1)}, u32[]{:S(2)}, u32[]{:S(2)}) collective-permute-start(bf16[128,1024]{1,0:T(8,128)(2,1)S(1)} %get-tuple-element.48.refs_2_), channel_id=1, source_target_pairs={{0,1},{1,0},{2,3},{3,2},{4,5},{5,4},{6,7},{7,6},{8,9},{9,8},{10,11... | collective-permute-start | bytes 786440 | tf_op jit(solution)/shard_map/ppermute | solution.py:313
  276.7 33.3 %collective-permute-start.12 = (bf16[64,1024]{1,0:T(8,128)(2,1)S(1)}, bf16[64,1024]{1,0:T(8,128)(2,1)S(1)}, u32[]{:S(2)}, u32[]{:S(2)}) collective-permute-start(bf16[64,1024]{1,0:T(8,128)(2,1)S(1)} %get-tuple-element.52), channel_id=1, source_target_pairs={{0,1},{1,0},{2,3},{3,2},{4,5},{5,4},{6,7},{7,6},{8,9},{9,8},{10,11... | collective-permute-start | bytes 393224 | tf_op jit(solution)/shard_map/ppermute | solution.py:313
  277.1 34.3 %collective-permute-start.10 = (bf16[32,1024]{1,0:T(8,128)(2,1)S(1)}, bf16[32,1024]{1,0:T(8,128)(2,1)S(1)}, u32[]{:S(2)}, u32[]{:S(2)}) collective-permute-start(bf16[32,1024]{1,0:T(8,128)(2,1)S(1)} %get-tuple-element.50), channel_id=1, source_target_pairs={{0,1},{1,0},{2,3},{3,2},{4,5},{5,4},{6,7},{7,6},{8,9},{9,8},{10,11... | collective-permute-start | bytes 196616 | tf_op jit(solution)/shard_map/ppermute | solution.py:313
  278.8 31.9 %collective-permute-start.11 = (bf16[32,1024]{1,0:T(8,128)(2,1)S(1)}, bf16[32,1024]{1,0:T(8,128)(2,1)S(1)}, u32[]{:S(2)}, u32[]{:S(2)}) collective-permute-start(bf16[32,1024]{1,0:T(8,128)(2,1)S(1)} %get-tuple-element.51), channel_id=1, source_target_pairs={{0,1},{1,0},{2,3},{3,2},{4,5},{5,4},{6,7},{7,6},{8,9},{9,8},{10,11... | collective-permute-start | bytes 196616 | tf_op jit(solution)/shard_map/ppermute | solution.py:313

commit v6 on v5

--- a/solution.py
+++ b/solution.py
@@ -12,12 +12,13 @@
 PAIR = ((0, 1), (1, 0))
 ANY = pl.BlockSpec(memory_space=pl.ANY)
 VMEM = pl.BlockSpec(memory_space=pltpu.VMEM)
-EARLY = 80
-HEAD, NEXT = 3, 5
+PARTS = (40, 48)
+EARLY = sum(PARTS)
+HEAD, NEXT = 2, 6
 LONG = 8
 AHEAD = 12
 LAST = (64, 32, 32)
-LEAST = 40
+LEAST = 42
 
 
 def cost(us):
@@ -63,8 +64,11 @@
         for cols in lane_tiles(m_ref):
             v = merged_tile(m_ref, s_ref, block_rows(b), cols)
             merged_ref[block_rows(b), cols] = v
-            if early and b == 0:
-                refs[2][:, cols] = v[:early].astype(jnp.bfloat16)
+            at = 0
+            for early_ref in refs[2 : 2 + len(early)] if b == 0 else ():
+                rows = early_ref.shape[0]
+                early_ref[:, cols] = v[at : at + rows].astype(jnp.bfloat16)
+                at += rows
             acc = acc + v * v
         sums_ref[b] = jnp.sum(acc.T, axis=0, keepdims=True)
 
@@ -114,12 +118,11 @@
     copy.wait()
 
 
-def place_early_kernel(recv_ref, own_ref, other_ref, _, out_ref, held_ref, sem):
-    rows = recv_ref.shape[0]
-    inverse = row_scales(own_ref[0], other_ref[0])[:rows]
+def place_early_kernel(row, recv_ref, own_ref, other_ref, _, out_ref, held_ref, sem):
+    inverse = row_scales(own_ref[0], other_ref[0])[row : row + recv_ref.shape[0]]
     for cols in lane_tiles(recv_ref):
         held_ref[:, cols] = (recv_ref[:, cols].astype(jnp.float32) * inverse).astype(jnp.bfloat16)
-    copy = pltpu.make_async_copy(held_ref, received_half(out_ref, 0, recv_ref.shape), sem)
+    copy = pltpu.make_async_copy(held_ref, received_half(out_ref, row, recv_ref.shape), sem)
     copy.start()
     copy.wait()
 
@@ -162,7 +165,7 @@
 def head_of(m, s, first, blocks, early, after=()):
     rows, width = blocks * LANES, m.shape[1]
     shapes = [sums_shape(blocks), jax.ShapeDtypeStruct((rows, width), jnp.float32)]
-    shapes += [jax.ShapeDtypeStruct((early, width), jnp.bfloat16)] if early else []
+    shapes += [jax.ShapeDtypeStruct((rows, width), jnp.bfloat16) for rows in early]
     return pl.pallas_call(
         after_of(functools.partial(head_kernel, first, early), 2, len(after)),
         in_specs=[ANY, ANY] + [ANY] * len(after),
@@ -295,9 +298,9 @@
     )(recv, out)
 
 
-def place_early(recv, own, other, out):
-    return pl.pallas_call(
-        place_early_kernel,
+def place_early(recv, own, other, out, row):
+    return pl.pallas_call(
+        functools.partial(place_early_kernel, row),
         in_specs=[VMEM, VMEM, VMEM, ANY],
         out_specs=ANY,
         out_shape=jax.ShapeDtypeStruct(out.shape, out.dtype),
@@ -331,13 +334,13 @@
     head, near = HEAD * LANES, (HEAD + NEXT) * LANES
     recvs = []
 
-    own0, merged0, early = head_of(m, s, 0, HEAD, EARLY)
+    own0, merged0, *early = head_of(m, s, 0, HEAD, PARTS)
+    other_early = [swap(x) for x in early]
     sums0 = own0, swap(own0)
-    other_early = swap(early)
-    half = EARLY + (head - EARLY) // 32 * 16
+    half = EARLY + (head - EARLY) * 2 // 3 // 16 * 16
     send_a, send_b = head_norm_of(merged0, *sums0, ((EARLY, half - EARLY), (half, head - half)))
     recvs.append((EARLY, swap(send_a)))
-    own1, merged1 = head_of(m, s, head, NEXT, 0, (send_a,))
+    own1, merged1 = head_of(m, s, head, NEXT, (), (send_a,))
     sums1 = own1, swap(own1)
     recvs.append((half, swap(send_b)))
 
@@ -358,7 +361,10 @@
         if recvs[0][0] == EARLY:
             _, out = norm_of(m, s, *sums0, 0, 0, head, out)
             _, out = norm_of(m, s, *sums1, head, head, near - head, out)
-            out = place_early(other_early, *sums0, out)
+            at = 0
+            for recv in other_early:
+                out = place_early(recv, *sums0, out, at)
+                at += recv.shape[0]
         while recvs and sum(recv.shape[0] for _, recv in recvs[1:]) >= ahead:
             at, recv = recvs.pop(0)
             out = place(recv, out, at)
@@ -376,7 +382,7 @@
     for rows in LAST:
         cuts.append((at, rows))
         at += rows
-    _, merged = head_of(m, s, n - LANES, 1, 0, (send,))
+    _, merged = head_of(m, s, n - LANES, 1, (), (send,))
     sends = head_norm_of(merged, *(x[-1:] for x in sums2), tuple(cuts))
     for (at, _), send in zip(cuts, sends, strict=True):
         recvs.append((n - LANES + at, swap(send)))

time: 313 us -> 327 us (1.045)
  waiting for transfers between devices: 193 us -> 207 us
    ppermute x19 -> x20, waiting for transfers between devices: 193 us -> 207 us  [swap(): return lax.ppermute(x, 'zero', PAIR)]
    ppermute x19 -> x20, starting transfers between devices: 27.3 us -> 26.9 us  [swap(): return lax.ppermute(x, 'zero', PAIR)]
  transfers between devices with their start and end apart: 19 -> 20, of which waited for: 7 -> 7; matrix products, arithmetic and copies ran while one was open for 0% -> 0% of each run, Pallas kernels for 15% -> 15%
where the time goes in v6:
time: 327 us
  waiting for transfers between devices  207 us (63%)
  Pallas kernels  69.6 us (21%)
  starting transfers between devices  26.9 us (8%)
  blocking collectives  22.3 us (7%)
    ppermute x20, waiting for transfers between devices, swap(): return lax.ppermute(x, 'zero', PAIR)  207 us
    pallas_call x10, Pallas kernels, norm_of(): pl.pallas_call(norm_kernel, grid=(count // rows,), in_specs=[block, block...  34.2 us
    ppermute x20, starting transfers between devices, swap(): return lax.ppermute(x, 'zero', PAIR)  26.9 us
    all_gather x1, blocking collectives, pair_steps(): serve_router = router_of(lax.all_gather(rows, 'bank')).T  22.3 us
    pallas_call x14, Pallas kernels, place(): pl.pallas_call(functools.partial(place_kernel, row), in_specs=[VMEM, ANY]...  14.2 us
    pallas_call x1, Pallas kernels, sums_of(): pl.pallas_call(after_of(sums_kernel, 2, 1), grid=(count // rows,), in_spe...  11.7 us
  transfers between devices with their start and end apart: 20, of which 7 were waited for; matrix products, arithmetic and copies ran while one was open for 0% of the time, Pallas kernels for 15%

profile of v6, /device:TPU:0, one launch (start us, length us, event | category | flops | bytes accessed | tf_op | source)
XLA Modules:
  0.0 326.6 jit_solution(868833551980293774)
XLA Ops:
  0.6 1.5 head.3
  2.2 3.1 collective-permute-start
  5.2 1.6 collective-permute-done.other_ref.refs_1_
  6.9 2.5 head.4
  9.5 2.1 collective-permute-start.1
  11.6 1.6 collective-permute-done.1.other_ref.refs_3_
  13.4 11.7 %sums.1.own_ref.refs_4_ = f32[36,1,128]{2,1,0:T(1,128)S(1)} custom-call(f32[5632,1024]{1,0:T(8,128)} %bitcast.11, bf16[5632,1024]{1,0:T(8,128)(2,1)} %bitcast.25, bf16[384,1024]{1,0:T(8,128)(2,1)S(1)} %head_norm.5.refs_2_), custom_call_target="tpu_custom_call" | custom-call | flops 9216000 | bytes 1024 | tf_op jit(solution)/shard_map/sums/pallas_call | solution.py:253
  25.1 2.1 collective-permute-start.2
  27.2 1.7 collective-permute-done.2.other_ref.refs_5_
  28.9 4.1 %norm.10 = (bf16[1024,1024]{1,0:T(8,128)(2,1)S(1)}, bf16[5632,2048]{1,0:T(8,128)(2,1)}) custom-call(f32[5632,1024]{1,0:T(8,128)} %bitcast.12, bf16[5632,1024]{1,0:T(8,128)(2,1)} %bitcast.26, f32[36,1,128]{2,1,0:T(1,128)S(1)} %sums.1.own_ref.refs_4_, f32[36,1,128]{2,1,0:T(1,128)S(1)} %collective-permute-done.2.other_ref.refs_5_), custom_call_target="tpu_custom_call" | custom-call | flops 3072000 | bytes 1024 | tf_op jit(solution)/shard_map/norm/pallas_call | solution.py:271
  33.0 2.0 collective-permute-start.4
  35.3 2.1 collective-permute-start.5
  37.4 4.5 %norm.11 = (bf16[1024,1024]{1,0:T(8,128)(2,1)}, bf16[5632,2048]{1,0:T(8,128)(2,1)}) custom-call(f32[5632,1024]{1,0:T(8,128)} %bitcast.13, bf16[5632,1024]{1,0:T(8,128)(2,1)} %bitcast.27, f32[36,1,128]{2,1,0:T(1,128)S(1)} %sums.1.own_ref.refs_4_, f32[36,1,128]{2,1,0:T(1,128)S(1)} %collective-permute-done.2.other_ref.refs_5_, ...), custom_call_target="tpu_custom_call", output_to_operand_aliasing={{1}: (4, {})} | custom-call | flops 3072000 | bytes 1024 | tf_op jit(solution)/shard_map/norm/pallas_call | solution.py:271
  41.9 2.0 collective-permute-start.10
  43.9 114.8 %collective-permute-done.10.recv_ref = bf16[40,1024]{1,0:T(8,128)(2,1)S(1)} collective-permute-done((bf16[40,1024]{1,0:T(8,128)(2,1)S(1)}, bf16[40,1024]{1,0:T(8,128)(2,1)S(1)}, u32[]{:S(2)}, u32[]{:S(2)}) %collective-permute-start.10) | collective-permute-done | bytes 81952 | tf_op jit(solution)/shard_map/ppermute | solution.py:316
  158.7 1.7 collective-permute-start.9
  160.4 3.9 %collective-permute-done.9.recv_ref = bf16[48,1024]{1,0:T(8,128)(2,1)S(1)} collective-permute-done((bf16[48,1024]{1,0:T(8,128)(2,1)S(1)}, bf16[48,1024]{1,0:T(8,128)(2,1)S(1)}, u32[]{:S(2)}, u32[]{:S(2)}) %collective-permute-start.9) | collective-permute-done | bytes 98336 | tf_op jit(solution)/shard_map/ppermute | solution.py:316
  164.4 1.6 collective-permute-start.8
  165.9 4.8 %collective-permute-done.8.recv_ref = bf16[112,1024]{1,0:T(8,128)(2,1)S(1)} collective-permute-done((bf16[112,1024]{1,0:T(8,128)(2,1)S(1)}, bf16[112,1024]{1,0:T(8,128)(2,1)S(1)}, u32[]{:S(2)}, u32[]{:S(2)}) %collective-permute-start.8) | collective-permute-done | bytes 229408 | tf_op jit(solution)/shard_map/ppermute | solution.py:316
  172.2 2.5 norm.12
  174.7 5.0 %norm.13 = (bf16[768,1024]{1,0:T(8,128)(2,1)}, bf16[5632,2048]{1,0:T(8,128)(2,1)}) custom-call(f32[5632,1024]{1,0:T(8,128)} %bitcast.15, bf16[5632,1024]{1,0:T(8,128)(2,1)} %bitcast.29, f32[6,1,128]{2,1,0:T(1,128)S(1)} %get-tuple-element.36.own_ref.refs_2_, ...), custom_call_target="tpu_custom_call", output_to_operand_aliasing={{1}: (4, {})} | custom-call | flops 2304000 | bytes 1024 | tf_op jit(solution)/shard_map/norm/pallas_call | solution.py:271
  184.4 4.2 %norm.14 = (bf16[1024,1024]{1,0:T(8,128)(2,1)S(1)}, bf16[5632,2048]{1,0:T(8,128)(2,1)}) custom-call(f32[5632,1024]{1,0:T(8,128)} %bitcast.16, bf16[5632,1024]{1,0:T(8,128)(2,1)} %bitcast.30, f32[36,1,128]{2,1,0:T(1,128)S(1)} %sums.1.own_ref.refs_4_, f32[36,1,128]{2,1,0:T(1,128)S(1)} %collective-permute-done.2.other_ref.refs_5_, ...), custom_call_target="tpu_custom_call", output_to_operand_aliasing={{1}: (4, {})} | custom-call | flops 3072000 | bytes 1024 | tf_op jit(solution)/shard_map/norm/pallas_call | solution.py:271
  190.6 4.4 %norm.15 = (bf16[768,1024]{1,0:T(8,128)(2,1)S(1)}, bf16[5632,2048]{1,0:T(8,128)(2,1)}) custom-call(f32[5632,1024]{1,0:T(8,128)} %bitcast.17, bf16[5632,1024]{1,0:T(8,128)(2,1)} %bitcast.31, f32[36,1,128]{2,1,0:T(1,128)S(1)} %sums.1.own_ref.refs_4_, f32[36,1,128]{2,1,0:T(1,128)S(1)} %collective-permute-done.2.other_ref.refs_5_, ...), custom_call_target="tpu_custom_call", output_to_operand_aliasing={{1}: (4, {})} | custom-call | flops 2304000 | bytes 1024 | tf_op jit(solution)/shard_map/norm/pallas_call | solution.py:271
  196.4 2.9 place.19.refs_0_
  199.4 3.5 %norm.16 = (bf16[384,1024]{1,0:T(8,128)(2,1)S(1)}, bf16[5632,2048]{1,0:T(8,128)(2,1)}) custom-call(f32[5632,1024]{1,0:T(8,128)} %bitcast.18, bf16[5632,1024]{1,0:T(8,128)(2,1)} %bitcast.32, f32[36,1,128]{2,1,0:T(1,128)S(1)} %sums.1.own_ref.refs_4_, f32[36,1,128]{2,1,0:T(1,128)S(1)} %collective-permute-done.2.other_ref.refs_5_, ...), custom_call_target="tpu_custom_call", output_to_operand_aliasing={{1}: (4, {})} | custom-call | flops 1152000 | bytes 1024 | tf_op jit(solution)/shard_map/norm/pallas_call | solution.py:271
  203.5 1.5 collective-permute-start.19
  205.0 2.0 norm.17
  207.5 2.0 norm.18
  209.5 78.3 %collective-permute-done.19.other_ref = bf16[4,1024]{1,0:T(4,128)(2,1)S(1)} collective-permute-done((bf16[4,1024]{1,0:T(4,128)(2,1)S(1)}, bf16[4,1024]{1,0:T(4,128)(2,1)S(1)}, u32[]{:S(2)}, u32[]{:S(2)}) %collective-permute-start.19) | collective-permute-done | bytes 8224 | tf_op jit(solution)/shard_map/ppermute | solution.py:316
  288.5 1.8 head.5
  293.9 22.3 %all-gather.1.gathered_ref = bf16[16,4,2048]{2,1,0:T(4,128)(2,1)S(1)} all-gather(bf16[1,4,2048]{2,1,0:T(4,128)(2,1)S(1)} %bitcast.7), channel_id=2, replica_groups=mesh['bank'=16,'zero'=2] {'bank'}, dimensions={0}, use_global_device_ids=true | all-gather | bytes 278528 | tf_op jit(solution)/shard_map/all_gather | solution.py:358
  317.7 2.1 norm.19
  (57 shorter events, 23.9 us)
Async XLA Ops:
  2.2 4.6 %collective-permute-start = (f32[2,1,128]{2,1,0:T(1,128)S(1)}, f32[2,1,128]{2,1,0:T(1,128)S(1)}, u32[]{:S(2)}, u32[]{:S(2)}) collective-permute-start(f32[2,1,128]{2,1,0:T(1,128)S(1)} %get-tuple-element.33.own_ref.refs_0_), channel_id=1, source_target_pairs={{0,1},{1,0},{2,3},{3,2},{4,5},{5,4},{6,7},{7,6},{8,9},{9,8},{10,11... | collective-permute-start | bytes 3080 | tf_op jit(solution)/shard_map/ppermute | solution.py:316
  6.8 173.6 %copy-start = (f32[2,1,128]{2,1,0:T(1,128)}, f32[2,1,128]{2,1,0:T(1,128)S(1)}, u32[]{:S(2)}) copy-start(f32[2,1,128]{2,1,0:T(1,128)S(1)} %collective-permute-done.other_ref.refs_1_) | copy-start | bytes 3076
  9.5 3.7 %collective-permute-start.1 = (f32[6,1,128]{2,1,0:T(1,128)S(1)}, f32[6,1,128]{2,1,0:T(1,128)S(1)}, u32[]{:S(2)}, u32[]{:S(2)}) collective-permute-start(f32[6,1,128]{2,1,0:T(1,128)S(1)} %get-tuple-element.36.own_ref.refs_2_), channel_id=1, source_target_pairs={{0,1},{1,0},{2,3},{3,2},{4,5},{5,4},{6,7},{7,6},{8,9},{9,8},{10,11... | collective-permute-start | bytes 9224 | tf_op jit(solution)/shard_map/ppermute | solution.py:316
  25.1 3.8 %collective-permute-start.2 = (f32[36,1,128]{2,1,0:T(1,128)S(1)}, f32[36,1,128]{2,1,0:T(1,128)S(1)}, u32[]{:S(2)}, u32[]{:S(2)}) collective-permute-start(f32[36,1,128]{2,1,0:T(1,128)S(1)} %sums.1.own_ref.refs_4_), channel_id=1, source_target_pairs={{0,1},{1,0},{2,3},{3,2},{4,5},{5,4},{6,7},{7,6},{8,9},{9,8},{10,11... | collective-permute-start | bytes 55304 | tf_op jit(solution)/shard_map/ppermute | solution.py:316
  33.0 156.2 %collective-permute-start.4 = (bf16[1024,1024]{1,0:T(8,128)(2,1)S(1)}, bf16[1024,1024]{1,0:T(8,128)(2,1)S(1)}, u32[]{:S(2)}, u32[]{:S(2)}) collective-permute-start(bf16[1024,1024]{1,0:T(8,128)(2,1)S(1)} %get-tuple-element.39), channel_id=1, source_target_pairs={{0,1},{1,0},{2,3},{3,2},{4,5},{5,4},{6,7},{7,6},{8,9},{9,8},{10,11... | collective-permute-start | bytes 6291464 | tf_op jit(solution)/shard_map/ppermute | solution.py:316
  35.1 147.6 %collective-permute-start.6 = (bf16[384,1024]{1,0:T(8,128)(2,1)S(1)}, bf16[384,1024]{1,0:T(8,128)(2,1)S(1)}, u32[]{:S(2)}, u32[]{:S(2)}) collective-permute-start(bf16[384,1024]{1,0:T(8,128)(2,1)S(1)} %head_norm.5.refs_2_), channel_id=1, source_target_pairs={{0,1},{1,0},{2,3},{3,2},{4,5},{5,4},{6,7},{7,6},{8,9},{9,8},{10,11... | collective-permute-start | bytes 2359304 | tf_op jit(solution)/shard_map/ppermute | solution.py:316
  35.3 148.2 %collective-permute-start.5 = (bf16[384,1024]{1,0:T(8,128)(2,1)S(1)}, bf16[384,1024]{1,0:T(8,128)(2,1)S(1)}, u32[]{:S(2)}, u32[]{:S(2)}) collective-permute-start(bf16[384,1024]{1,0:T(8,128)(2,1)S(1)} %head_norm.6), channel_id=1, source_target_pairs={{0,1},{1,0},{2,3},{3,2},{4,5},{5,4},{6,7},{7,6},{8,9},{9,8},{10,11... | collective-permute-start | bytes 2359304 | tf_op jit(solution)/shard_map/ppermute | solution.py:316
  41.8 154.6 %collective-permute-start.3 = (bf16[1024,1024]{1,0:T(8,128)(2,1)}, bf16[1024,1024]{1,0:T(8,128)(2,1)}, u32[]{:S(2)}, u32[]{:S(2)}) collective-permute-start(bf16[1024,1024]{1,0:T(8,128)(2,1)} %get-tuple-element.38), channel_id=1, source_target_pairs={{0,1},{1,0},{2,3},{3,2},{4,5},{5,4},{6,7},{7,6},{8,9},{9,8},{10,11... | collective-permute-start | bytes 6291464 | tf_op jit(solution)/shard_map/ppermute | solution.py:316
  41.9 116.8 %collective-permute-start.10 = (bf16[40,1024]{1,0:T(8,128)(2,1)S(1)}, bf16[40,1024]{1,0:T(8,128)(2,1)S(1)}, u32[]{:S(2)}, u32[]{:S(2)}) collective-permute-start(bf16[40,1024]{1,0:T(8,128)(2,1)S(1)} %get-tuple-element.42), channel_id=1, source_target_pairs={{0,1},{1,0},{2,3},{3,2},{4,5},{5,4},{6,7},{7,6},{8,9},{9,8},{10,11... | collective-permute-start | bytes 245768 | tf_op jit(solution)/shard_map/ppermute | solution.py:316
  158.7 5.7 %collective-permute-start.9 = (bf16[48,1024]{1,0:T(8,128)(2,1)S(1)}, bf16[48,1024]{1,0:T(8,128)(2,1)S(1)}, u32[]{:S(2)}, u32[]{:S(2)}) collective-permute-start(bf16[48,1024]{1,0:T(8,128)(2,1)S(1)} %get-tuple-element.41), channel_id=1, source_target_pairs={{0,1},{1,0},{2,3},{3,2},{4,5},{5,4},{6,7},{7,6},{8,9},{9,8},{10,11... | collective-permute-start | bytes 294920 | tf_op jit(solution)/shard_map/ppermute | solution.py:316
  164.4 6.4 %collective-permute-start.8 = (bf16[112,1024]{1,0:T(8,128)(2,1)S(1)}, bf16[112,1024]{1,0:T(8,128)(2,1)S(1)}, u32[]{:S(2)}, u32[]{:S(2)}) collective-permute-start(bf16[112,1024]{1,0:T(8,128)(2,1)S(1)} %get-tuple-element.34.refs_2_), channel_id=1, source_target_pairs={{0,1},{1,0},{2,3},{3,2},{4,5},{5,4},{6,7},{7,6},{8,9},{9,8},{10,11... | collective-permute-start | bytes 688136 | tf_op jit(solution)/shard_map/ppermute | solution.py:316
  170.8 11.2 %collective-permute-start.7 = (bf16[56,1024]{1,0:T(8,128)(2,1)S(1)}, bf16[56,1024]{1,0:T(8,128)(2,1)S(1)}, u32[]{:S(2)}, u32[]{:S(2)}) collective-permute-start(bf16[56,1024]{1,0:T(8,128)(2,1)S(1)} %get-tuple-element.40), channel_id=1, source_target_pairs={{0,1},{1,0},{2,3},{3,2},{4,5},{5,4},{6,7},{7,6},{8,9},{9,8},{10,11... | collective-permute-start | bytes 344072 | tf_op jit(solution)/shard_map/ppermute | solution.py:316
  188.6 101.8 %collective-permute-start.18 = (bf16[1024,1024]{1,0:T(8,128)(2,1)S(1)}, bf16[1024,1024]{1,0:T(8,128)(2,1)S(1)}, u32[]{:S(2)}, u32[]{:S(2)}) collective-permute-start(bf16[1024,1024]{1,0:T(8,128)(2,1)S(1)} %get-tuple-element.58), channel_id=1, source_target_pairs={{0,1},{1,0},{2,3},{3,2},{4,5},{5,4},{6,7},{7,6},{8,9},{9,8},{10,11... | collective-permute-start | bytes 6291464 | tf_op jit(solution)/shard_map/ppermute | solution.py:316
  195.0 97.5 %collective-permute-start.17 = (bf16[768,1024]{1,0:T(8,128)(2,1)S(1)}, bf16[768,1024]{1,0:T(8,128)(2,1)S(1)}, u32[]{:S(2)}, u32[]{:S(2)}) collective-permute-start(bf16[768,1024]{1,0:T(8,128)(2,1)S(1)} %get-tuple-element.57), channel_id=1, source_target_pairs={{0,1},{1,0},{2,3},{3,2},{4,5},{5,4},{6,7},{7,6},{8,9},{9,8},{10,11... | collective-permute-start | bytes 4718600 | tf_op jit(solution)/shard_map/ppermute | solution.py:316
  199.3 4.1 %copy-start.2 = (f32[1024,4]{0,1:T(4,128)S(1)}, f32[1024,4]{0,1:T(4,128)}, u32[]{:S(2)}) copy-start(f32[1024,4]{0,1:T(4,128)} %param.6) | copy-start | bytes 49156
  199.4 4.1 %copy-start.3 = (f32[1024]{0:T(1024)S(1)}, f32[1024]{0:T(1024)}, u32[]{:S(2)}) copy-start(f32[1024]{0:T(1024)} %param.7) | copy-start | bytes 12292
  202.8 89.0 %collective-permute-start.16 = (bf16[384,1024]{1,0:T(8,128)(2,1)S(1)}, bf16[384,1024]{1,0:T(8,128)(2,1)S(1)}, u32[]{:S(2)}, u32[]{:S(2)}) collective-permute-start(bf16[384,1024]{1,0:T(8,128)(2,1)S(1)} %get-tuple-element.56), channel_id=1, source_target_pairs={{0,1},{1,0},{2,3},{3,2},{4,5},{5,4},{6,7},{7,6},{8,9},{9,8},{10,11... | collective-permute-start | bytes 2359304 | tf_op jit(solution)/shard_map/ppermute | solution.py:316
  203.5 84.4 %collective-permute-start.19 = (bf16[4,1024]{1,0:T(4,128)(2,1)S(1)}, bf16[4,1024]{1,0:T(4,128)(2,1)S(1)}, u32[]{:S(2)}, u32[]{:S(2)}) collective-permute-start(bf16[4,1024]{1,0:T(4,128)(2,1)S(1)} %fusion.own_ref), channel_id=1, source_target_pairs={{0,1},{1,0},{2,3},{3,2},{4,5},{5,4},{6,7},{7,6},{8,9},{9,8},{10,11... | collective-permute-start | bytes 24584 | tf_op jit(solution)/shard_map/ppermute | solution.py:316
  206.9 116.2 %collective-permute-start.15 = (bf16[128,1024]{1,0:T(8,128)(2,1)S(1)}, bf16[128,1024]{1,0:T(8,128)(2,1)S(1)}, u32[]{:S(2)}, u32[]{:S(2)}) collective-permute-start(bf16[128,1024]{1,0:T(8,128)(2,1)S(1)} %get-tuple-element.55), channel_id=1, source_target_pairs={{0,1},{1,0},{2,3},{3,2},{4,5},{5,4},{6,7},{7,6},{8,9},{9,8},{10,11... | collective-permute-start | bytes 786440 | tf_op jit(solution)/shard_map/ppermute | solution.py:316
  209.5 107.5 %copy-start.1 = (f32[2,1,128]{2,1,0:T(1,128)S(1)}, f32[2,1,128]{2,1,0:T(1,128)}, u32[]{:S(2)}) copy-start(f32[2,1,128]{2,1,0:T(1,128)} %copy-done) | copy-start | bytes 3076
  287.8 36.0 %collective-permute-start.14 = (bf16[128,1024]{1,0:T(8,128)(2,1)S(1)}, bf16[128,1024]{1,0:T(8,128)(2,1)S(1)}, u32[]{:S(2)}, u32[]{:S(2)}) collective-permute-start(bf16[128,1024]{1,0:T(8,128)(2,1)S(1)} %get-tuple-element.50.refs_2_), channel_id=1, source_target_pairs={{0,1},{1,0},{2,3},{3,2},{4,5},{5,4},{6,7},{7,6},{8,9},{9,8},{10,11... | collective-permute-start | bytes 786440 | tf_op jit(solution)/shard_map/ppermute | solution.py:316
  290.4 34.2 %collective-permute-start.13 = (bf16[64,1024]{1,0:T(8,128)(2,1)S(1)}, bf16[64,1024]{1,0:T(8,128)(2,1)S(1)}, u32[]{:S(2)}, u32[]{:S(2)}) collective-permute-start(bf16[64,1024]{1,0:T(8,128)(2,1)S(1)} %get-tuple-element.54), channel_id=1, source_target_pairs={{0,1},{1,0},{2,3},{3,2},{4,5},{5,4},{6,7},{7,6},{8,9},{9,8},{10,11... | collective-permute-start | bytes 393224 | tf_op jit(solution)/shard_map/ppermute | solution.py:316
  291.9 34.1 %collective-permute-start.11 = (bf16[32,1024]{1,0:T(8,128)(2,1)S(1)}, bf16[32,1024]{1,0:T(8,128)(2,1)S(1)}, u32[]{:S(2)}, u32[]{:S(2)}) collective-permute-start(bf16[32,1024]{1,0:T(8,128)(2,1)S(1)} %get-tuple-element.52), channel_id=1, source_target_pairs={{0,1},{1,0},{2,3},{3,2},{4,5},{5,4},{6,7},{7,6},{8,9},{9,8},{10,11... | collective-permute-start | bytes 196616 | tf_op jit(solution)/shard_map/ppermute | solution.py:316
  292.5 32.8 %collective-permute-start.12 = (bf16[32,1024]{1,0:T(8,128)(2,1)S(1)}, bf16[32,1024]{1,0:T(8,128)(2,1)S(1)}, u32[]{:S(2)}, u32[]{:S(2)}) collective-permute-start(bf16[32,1024]{1,0:T(8,128)(2,1)S(1)} %get-tuple-element.53), channel_id=1, source_target_pairs={{0,1},{1,0},{2,3},{3,2},{4,5},{5,4},{6,7},{7,6},{8,9},{9,8},{10,11... | collective-permute-start | bytes 196616 | tf_op jit(solution)/shard_map/ppermute | solution.py:316
